TPU v7x, 8 devices: a whole 2x2x1 slice. The times are simulated.
8 devices in a mesh: rep: 1 (over z), ep: 2 (over y), fsdp: 4 (over x, core).
Axes of the slice: x: 2, y: 2, z: 1, core: 2. Of those that a mesh axis runs over, the one named last changes fastest.
Arguments:
- x_in: bfloat16 [16384, 2048], P(('rep', 'ep', 'fsdp'))
- norm_w: float32 [2, 2048], replicated
- router_w: bfloat16 [2, 2048, 4], replicated
- gate_w: bfloat16 [2, 4, 2048, 5632], P(None, 'ep', None, 'fsdp')
- up_w: bfloat16 [2, 4, 2048, 5632], P(None, 'ep', None, 'fsdp')
- down_w: bfloat16 [2, 4, 5632, 2048], P(None, 'ep', 'fsdp')
- routes: int32 [2, 16384, 2], P(None, ('rep', 'ep', 'fsdp'))
Outputs:
- output: bfloat16 [16384, 2048], P(('rep', 'ep', 'fsdp'))
All inputs are finite; a program needn't handle non-finite values.
Results may differ from a plain program's by a relative error of at most 0.0124657.
Values are sent between devices in bfloat16 or wider.
A program may use at most 1 GiB of HBM per device.

v0:
```python
import jax
import jax.numpy as jnp
from jax import lax
from jax.sharding import PartitionSpec as P

NORM_EPS = 1e-5


def rms_norm(stream, norm_row):
    widened = stream.astype(jnp.float32)
    inv_rms = lax.rsqrt(jnp.mean(widened * widened, axis=-1, keepdims=True) + NORM_EPS)
    return (widened * inv_rms * norm_row).astype(jnp.bfloat16)


def route_gates(hidden, router_l, routes_l):
    logits = jnp.dot(hidden, router_l, preferred_element_type=jnp.float32)
    return jax.nn.softmax(jnp.take_along_axis(logits, routes_l, axis=-1), axis=-1)


def capacity_of(tok_dev, top_k, experts):
    return 8 * ((2 * tok_dev * top_k + 8 * experts - 1) // (8 * experts))


def slot_plan(routes_l, experts, capacity, owners):
    tok_dev, top_k = routes_l.shape
    flat_ids = routes_l.reshape(-1)
    onehot = (flat_ids[:, None] == jnp.arange(experts, dtype=flat_ids.dtype)[None, :]).astype(jnp.int32)
    pair_rank = jnp.sum((jnp.cumsum(onehot, axis=0) - 1) * onehot, axis=1)
    n_local = experts // owners
    pair_slot = ((flat_ids % n_local) * owners + flat_ids // n_local) * capacity + pair_rank
    pair_token = jnp.arange(tok_dev * top_k, dtype=jnp.int32) // top_k
    slot_token = jnp.zeros((experts * capacity,), jnp.int32).at[pair_slot].set(pair_token)
    return pair_slot, slot_token


def expert_ffn(expert_rows, gate_full, up_full, down_full):
    pre_gate = jnp.einsum("erd,edf->erf", expert_rows, gate_full, preferred_element_type=jnp.float32)
    pre_up = jnp.einsum("erd,edf->erf", expert_rows, up_full, preferred_element_type=jnp.float32)
    inner_act = (jax.nn.silu(pre_gate) * pre_up).astype(jnp.bfloat16)
    return jnp.einsum("erf,efd->erd", inner_act, down_full, preferred_element_type=jnp.float32).astype(jnp.bfloat16)


def combine(stream, gate_probs, pair_out):
    mixed_sum = jnp.sum(gate_probs[..., None] * pair_out.astype(jnp.float32), axis=-2)
    return (stream.astype(jnp.float32) + mixed_sum).astype(jnp.bfloat16)


def solution(mesh):
    owners = mesh.shape["ep"]
    token_spec = P(("rep", "ep", "fsdp"), None)
    expert_in_spec = P(None, "ep", None, "fsdp")
    expert_out_spec = P(None, "ep", "fsdp", None)
    route_spec = P(None, ("rep", "ep", "fsdp"), None)

    def device_step(x_in, norm_w, router_w, gate_w, up_w, down_w, routes):
        layers, tok_dev, top_k = routes.shape
        experts = router_w.shape[2]
        n_local = gate_w.shape[1]
        d_model = x_in.shape[1]
        capacity = capacity_of(tok_dev, top_k, experts)
        stream = x_in
        for layer_idx in range(layers):
            routes_l = routes[layer_idx]
            hidden = rms_norm(stream, norm_w[layer_idx])
            gate_probs = route_gates(hidden, router_w[layer_idx], routes_l)
            pair_slot, slot_token = slot_plan(routes_l, experts, capacity, owners)
            send_buf = hidden[slot_token].reshape(n_local, owners, capacity, d_model)
            recv_buf = lax.all_to_all(send_buf, "ep", 1, 1, tiled=True)
            gate_full = lax.all_gather(gate_w[layer_idx], "fsdp", axis=2, tiled=True)
            up_full = lax.all_gather(up_w[layer_idx], "fsdp", axis=2, tiled=True)
            down_full = lax.all_gather(down_w[layer_idx], "fsdp", axis=1, tiled=True)
            expert_out = expert_ffn(recv_buf.reshape(n_local, owners * capacity, d_model), gate_full, up_full, down_full)
            back_buf = lax.all_to_all(expert_out.reshape(n_local, owners, capacity, d_model), "ep", 1, 1, tiled=True)
            pair_out = back_buf.reshape(experts * capacity, d_model)[pair_slot].reshape(tok_dev, top_k, d_model)
            stream = combine(stream, gate_probs, pair_out)
        return stream

    return jax.shard_map(device_step, mesh=mesh,
                         in_specs=(token_spec, P(), P(), expert_in_spec, expert_in_spec, expert_out_spec, route_spec),
                         out_specs=token_spec, check_vma=False)
```

profile of v0, /device:TPU:0, one launch (start us, length us, event | category | flops | bytes accessed | tf_op | source)
XLA Modules:
  0.0 3614.2 jit_solution(16093351344322504570)
XLA Ops:
  6.5 16.0 fusion.60
  22.6 19.9 fusion.61
  42.6 19.9 fusion.62
  65.7 1.2 reduce-window.14
  67.6 15.5 scatter_custom_fusion
  83.2 5.1 fusion.18
  88.9 8.8 fusion.20
  97.7 65.8 %gather_fusion = bf16[8192,2048]{1,0:T(8,128)(2,1)} fusion(bf16[2048,2048]{1,0:T(8,128)(2,1)} %fusion.20, s32[8192]{0:T(1024)S(1)} %fusion.36), kind=kCustom, calls=%fused_computation.2 | custom fusion | bytes 67141632 | tf_op jit(solution)/shard_map/gather | solution.py:67
  163.5 23.1 copy.13
  186.6 13.0 all-to-all-start
  200.2 363.6 %all-to-all-done = bf16[2,2,2048,2048]{3,2,0,1:T(8,128)(2,1)} async-done(((bf16[2,2,2048,2048]{3,2,0,1:T(8,128)(2,1)}), bf16[2,2,2048,2048]{3,2,0,1:T(8,128)(2,1)}, u32[]{:S(2)}, u32[]{:S(2)}) %all-to-all-start) | async-done | bytes 33554464 | tf_op jit(solution)/shard_map/all_to_all | solution.py:68
  563.8 27.6 copy.14
  591.5 207.5 %fusion.10 = f32[2,4096,5632]{2,1,0:T(8,128)} fusion(bf16[2,4096,2048]{2,1,0:T(8,128)(2,1)} %bitcast.115, bf16[1,2,2048,5632]{3,2,1,0:T(8,128)(2,1)} %all-gather.13.cloned.1.call-done), kind=kOutput, calls=%fused_computation.20 | convolution fusion | flops 188978561024 | bytes 264241152 | tf_op jit(solution)/shard_map/erd,edf->erf/dot_general | solution.py:37
  799.0 204.4 %fusion.8 = f32[2,4096,5632]{2,1,0:T(8,128)} fusion(bf16[2,4096,2048]{2,1,0:T(8,128)(2,1)} %bitcast.116, bf16[1,2,2048,5632]{3,2,1,0:T(8,128)(2,1)} %all-gather.15.cloned.1.call-done), kind=kOutput, calls=%fused_computation.18 | convolution fusion | flops 188978561024 | bytes 264241152 | tf_op jit(solution)/shard_map/erd,edf->erf/dot_general | solution.py:38
  1003.4 235.9 %fusion.15 = bf16[2,4096,2048]{2,1,0:T(8,128)(2,1)} fusion(bf16[1,2,5632,2048]{3,2,1,0:T(8,128)(2,1)} %all-gather.17.cloned.1.call-done, f32[2,4096,5632]{2,1,0:T(8,128)} %fusion.8, f32[2,4096,5632]{2,1,0:T(8,128)} %fusion.10), kind=kOutput, calls=%fused_computation.31 | convolution fusion | flops 189272162304 | bytes 448790528 | tf_op jit(solution)/shard_map/erf,efd->erd/dot_general | solution.py:40
  1239.4 23.0 copy.15
  1262.3 13.4 all-to-all-start.1
  1276.2 1.1 eq.65
  1278.3 1.2 reshape_squeeze.7
  1280.3 5.6 fusion.46
  1286.0 34.7 gather_fusion.4
  1321.7 1.2 reduce-window.16
  1323.7 15.7 scatter_custom_fusion.1
  1341.5 295.8 %all-to-all-done.1 = bf16[2,2,2048,2048]{3,2,0,1:T(8,128)(2,1)} async-done(((bf16[2,2,2048,2048]{3,2,0,1:T(8,128)(2,1)}), bf16[2,2,2048,2048]{3,2,0,1:T(8,128)(2,1)}, u32[]{:S(2)}, u32[]{:S(2)}) %all-to-all-start.1) | async-done | bytes 33554464 | tf_op jit(solution)/shard_map/all_to_all | solution.py:73
  1637.3 22.9 copy.16
  1660.2 95.7 %gather_fusion.1 = bf16[4096,2048]{1,0:T(8,128)(2,1)} fusion(bf16[8192,2048]{1,0:T(8,128)(2,1)} %bitcast.111, s32[4096]{0:T(1024)S(1)} %broadcast_clamp_fusion.1), kind=kCustom, calls=%fused_computation.3 | custom fusion | bytes 33570816 | tf_op jit(solution)/shard_map/gather | solution.py:74
  1755.9 35.0 reshape.349
  1790.9 56.3 %multiply_reduce_fusion.1 = f32[2048,2048]{1,0:T(8,128)} fusion(f32[2048,2,2048]{2,1,0:T(2,128)} %reshape.349, f32[2048,2]{1,0:T(8,128)S(1)} %fusion.26), kind=kLoop, calls=%fused_computation.23 | loop fusion | flops 12582912 | bytes 50348032 | tf_op jit(solution)/shard_map/reduce_sum | solution.py:44
  1847.2 12.0 fusion.22
  1859.2 8.6 fusion.24
  1867.8 65.8 %gather_fusion.2 = bf16[8192,2048]{1,0:T(8,128)(2,1)} fusion(bf16[2048,2048]{1,0:T(8,128)(2,1)} %fusion.24, s32[8192]{0:T(1024)S(1)} %fusion.37), kind=kCustom, calls=%fused_computation.4 | custom fusion | bytes 67141632 | tf_op jit(solution)/shard_map/gather | solution.py:67
  1933.6 23.0 copy.18
  1956.6 13.0 all-to-all-start.2
  1970.1 360.1 %all-to-all-done.2 = bf16[2,2,2048,2048]{3,2,0,1:T(8,128)(2,1)} async-done(((bf16[2,2,2048,2048]{3,2,0,1:T(8,128)(2,1)}), bf16[2,2,2048,2048]{3,2,0,1:T(8,128)(2,1)}, u32[]{:S(2)}, u32[]{:S(2)}) %all-to-all-start.2) | async-done | bytes 33554464 | tf_op jit(solution)/shard_map/all_to_all | solution.py:68
  2330.2 23.3 copy.19
  2353.4 203.0 %fusion.5 = f32[2,4096,5632]{2,1,0:T(8,128)} fusion(bf16[2,4096,2048]{2,1,0:T(8,128)(2,1)} %bitcast.117, bf16[1,2,2048,5632]{3,2,1,0:T(8,128)(2,1)} %all-gather.19.cloned.1.call-done), kind=kOutput, calls=%fused_computation.15 | convolution fusion | flops 188978561024 | bytes 264241152 | tf_op jit(solution)/shard_map/erd,edf->erf/dot_general | solution.py:37
  2556.4 203.3 %fusion.3 = f32[2,4096,5632]{2,1,0:T(8,128)} fusion(bf16[2,4096,2048]{2,1,0:T(8,128)(2,1)} %bitcast.118, bf16[1,2,2048,5632]{3,2,1,0:T(8,128)(2,1)} %all-gather.21.cloned.1.call-done), kind=kOutput, calls=%fused_computation.13 | convolution fusion | flops 188978561024 | bytes 264241152 | tf_op jit(solution)/shard_map/erd,edf->erf/dot_general | solution.py:38
  2759.8 229.5 %fusion.12 = bf16[2,4096,2048]{2,1,0:T(8,128)(2,1)} fusion(bf16[1,2,5632,2048]{3,2,1,0:T(8,128)(2,1)} %all-gather.23.cloned.1.call-done, f32[2,4096,5632]{2,1,0:T(8,128)} %fusion.3, f32[2,4096,5632]{2,1,0:T(8,128)} %fusion.5), kind=kOutput, calls=%fused_computation.30 | convolution fusion | flops 189272162304 | bytes 448790528 | tf_op jit(solution)/shard_map/erf,efd->erd/dot_general | solution.py:40
  2989.2 23.0 copy.20
  3012.2 13.1 all-to-all-start.3
  3026.8 5.6 fusion.44
  3032.4 34.9 gather_fusion.5
  3070.1 315.0 %all-to-all-done.3 = bf16[2,2,2048,2048]{3,2,0,1:T(8,128)(2,1)} async-done(((bf16[2,2,2048,2048]{3,2,0,1:T(8,128)(2,1)}), bf16[2,2,2048,2048]{3,2,0,1:T(8,128)(2,1)}, u32[]{:S(2)}, u32[]{:S(2)}) %all-to-all-start.3) | async-done | bytes 33554464 | tf_op jit(solution)/shard_map/all_to_all | solution.py:73
  3385.1 22.9 copy.21
  3408.0 95.7 %gather_fusion.3 = bf16[4096,2048]{1,0:T(8,128)(2,1)} fusion(bf16[8192,2048]{1,0:T(8,128)(2,1)} %bitcast.112, s32[4096]{0:T(1024)S(1)} %copy-done.8), kind=kCustom, calls=%fused_computation.5 | custom fusion | bytes 33570816 | tf_op jit(solution)/shard_map/gather | solution.py:74
  3503.7 35.0 reshape.350
  3538.7 56.3 %multiply_reduce_fusion = f32[2048,2048]{1,0:T(8,128)} fusion(f32[2048,2,2048]{2,1,0:T(2,128)} %reshape.350, f32[2048,2]{1,0:T(8,128)S(1)} %fusion.28), kind=kLoop, calls=%fused_computation.22 | loop fusion | flops 12582912 | bytes 50348032 | tf_op jit(solution)/shard_map/reduce_sum | solution.py:44
  3595.0 12.0 fusion.25
  (99 shorter events, 16.0 us)
Async XLA Ops:
  6.5 584.9 %all-gather.13.cloned.1.call-start = ((), (), s32[]{:S(2)}) async-start(), calls=%async_computation.4 | async-start | bytes 57671680 | tf_op jit(solution)/shard_map/all_gather | solution.py:69
  22.5 776.4 %all-gather.15.cloned.1.call-start = ((), (), s32[]{:S(2)}) async-start(), calls=%async_computation.5 | async-start | bytes 57671680 | tf_op jit(solution)/shard_map/all_gather | solution.py:70
  42.6 20.6 copy-start.18
  42.6 45.8 %copy-start.19 = (f32[2,2048]{1,0:T(2,128)S(1)}, f32[2,2048]{1,0:T(2,128)}, u32[]{:S(2)}) copy-start(f32[2,2048]{1,0:T(2,128)} %param.10) | copy-start | bytes 49156
  42.6 960.9 %all-gather.17.cloned.1.call-start = ((), (), s32[]{:S(2)}) async-start(), calls=%async_computation.6 | async-start | bytes 57671680 | tf_op jit(solution)/shard_map/all_gather | solution.py:71
  62.5 2290.9 %all-gather.19.cloned.1.call-start = ((), (), s32[]{:S(2)}) async-start(), calls=%async_computation.7 | async-start | bytes 57671680 | tf_op jit(solution)/shard_map/all_gather | solution.py:69
  64.1 99.4 %copy-start.3 = (s32[1,2048,2]{2,1,0:T(8,128)}, s32[1,2048,2]{2,1,0:T(8,128)S(1)}, u32[]{:S(2)}) copy-start(s32[1,2048,2]{2,1,0:T(8,128)S(1)} %copy.22) | copy-start | bytes 49156
  67.3 96.2 %copy-start.20 = (s32[4096]{0:T(1024)}, s32[4096]{0:T(1024)S(1)}, u32[]{:S(2)}) copy-start(s32[4096]{0:T(1024)S(1)} %add_select_fusion) | copy-start | bytes 49156
  67.6 20.6 copy-start.11
  186.6 377.2 %all-to-all-start = ((bf16[2,2,2048,2048]{3,2,0,1:T(8,128)(2,1)}), bf16[2,2,2048,2048]{3,2,0,1:T(8,128)(2,1)}, u32[]{:S(2)}, u32[]{:S(2)}) async-start(bf16[2,2,2048,2048]{3,2,0,1:T(8,128)(2,1)} %copy.13), calls=%async_computation | async-start | bytes 67108864 | tf_op jit(solution)/shard_map/all_to_all | solution.py:68
  199.6 2356.8 %all-gather.21.cloned.1.call-start = ((), (), s32[]{:S(2)}) async-start(), calls=%async_computation.8 | async-start | bytes 57671680 | tf_op jit(solution)/shard_map/all_gather | solution.py:70
  1262.3 13.4 copy-start.9
  1262.3 17.2 copy-start.4
  1262.3 18.0 copy-start.16
  1262.3 374.9 %all-to-all-start.1 = ((bf16[2,2,2048,2048]{3,2,0,1:T(8,128)(2,1)}), bf16[2,2,2048,2048]{3,2,0,1:T(8,128)(2,1)}, u32[]{:S(2)}, u32[]{:S(2)}) async-start(bf16[2,2,2048,2048]{3,2,0,1:T(8,128)(2,1)} %copy.15), calls=%async_computation.1 | async-start | bytes 67108864 | tf_op jit(solution)/shard_map/all_to_all | solution.py:73
  1276.1 3.4 copy-start
  1286.0 35.7 copy-start.7
  1286.0 37.5 %copy-start.10 = (s32[4096]{0:T(1024)S(1)}, s32[4096]{0:T(1024)}, u32[]{:S(2)}) copy-start(s32[4096]{0:T(1024)} %eq.61) | copy-start | bytes 49156
  1286.0 37.5 %copy-start.6 = (s32[4096,1]{0,1:T(1,128)S(1)}, s32[4096,1]{0,1:T(1,128)}, u32[]{:S(2)}) copy-start(s32[4096,1]{0,1:T(1,128)} %reshape_squeeze.7) | copy-start | bytes 49156
  1286.0 53.4 %copy-start.12 = (s32[4096,1]{0,1:T(1,128)S(1)}, s32[4096,1]{0,1:T(1,128)}, u32[]{:S(2)}) copy-start(s32[4096,1]{0,1:T(1,128)} %copy-done.11) | copy-start | bytes 49156
  1286.0 53.5 %copy-start.5 = (s32[1,2048,2]{2,1,0:T(8,128)S(1)}, s32[1,2048,2]{2,1,0:T(8,128)}, u32[]{:S(2)}) copy-start(s32[1,2048,2]{2,1,0:T(8,128)} %copy-done.3) | copy-start | bytes 49156
  1323.7 15.7 copy-start.13
  1790.9 68.3 %copy-start.15 = (f32[1,2048]{1,0:T(1,128)S(1)}, f32[1,2048]{1,0:T(1,128)}, u32[]{:S(2)}) copy-start(f32[1,2048]{1,0:T(1,128)} %get-tuple-element.16) | copy-start | bytes 24580
  1956.6 373.6 %all-to-all-start.2 = ((bf16[2,2,2048,2048]{3,2,0,1:T(8,128)(2,1)}), bf16[2,2,2048,2048]{3,2,0,1:T(8,128)(2,1)}, u32[]{:S(2)}, u32[]{:S(2)}) async-start(bf16[2,2,2048,2048]{3,2,0,1:T(8,128)(2,1)} %copy.18), calls=%async_computation.2 | async-start | bytes 67108864 | tf_op jit(solution)/shard_map/all_to_all | solution.py:68
  1969.5 790.3 %all-gather.23.cloned.1.call-start = ((), (), s32[]{:S(2)}) async-start(), calls=%async_computation.9 | async-start | bytes 57671680 | tf_op jit(solution)/shard_map/all_gather | solution.py:71
  3012.2 13.1 copy-start.1
  3012.2 14.0 copy-start.14
  3012.2 14.6 copy-start.17
  3012.2 372.9 %all-to-all-start.3 = ((bf16[2,2,2048,2048]{3,2,0,1:T(8,128)(2,1)}), bf16[2,2,2048,2048]{3,2,0,1:T(8,128)(2,1)}, u32[]{:S(2)}, u32[]{:S(2)}) async-start(bf16[2,2,2048,2048]{3,2,0,1:T(8,128)(2,1)} %copy.20), calls=%async_computation.3 | async-start | bytes 67108864 | tf_op jit(solution)/shard_map/all_to_all | solution.py:73
  3032.4 35.9 copy-start.2
  3070.1 337.9 %copy-start.8 = (s32[4096]{0:T(1024)S(1)}, s32[4096]{0:T(1024)}, u32[]{:S(2)}) copy-start(s32[4096]{0:T(1024)} %broadcast_clamp_fusion) | copy-start | bytes 49156
Sparse Core Ops, SparseCore 0:
  22.7 273.3 all-gather.12
  297.6 270.5 all-gather.14
  569.8 271.8 all-gather.16
  843.1 270.5 all-gather.18
  1115.1 270.5 all-gather.20
  1971.6 273.3 all-gather.22
where the time goes:
time: 3630 us; the launch traced here: 3610 us
  waiting for transfers between devices  1340 us (37%)
  matrix products  1290 us (36%)
  local copies, waits for them, and re-layouts  749 us (21%)
  other arithmetic  167 us (5%)
  starting transfers between devices  52.9 us (1%)
    all_to_all x2, waiting for transfers between devices, device_step(): recv_buf = lax.all_to_all(send_buf, 'ep', 1, 1, tiled=True)  724 us
    all_to_all x2, waiting for transfers between devices, device_step(): lax.all_to_all(expert_out.reshape(n_local, owners, capacity, d_model), 'e...  611 us
    dot_general x2, matrix products, expert_ffn(): jnp.einsum('erf,efd->erd', inner_act, down_full, preferred_element_type=j...  465 us
    dot_general x2, matrix products, expert_ffn(): jnp.einsum('erd,edf->erf', expert_rows, gate_full, preferred_element_type...  411 us
    dot_general x2, matrix products, expert_ffn(): jnp.einsum('erd,edf->erf', expert_rows, up_full, preferred_element_type=j...  408 us
    gather x2, local copies, waits for them, and re-layouts, device_step(): back_buf.reshape(experts * capacity, d_model)[pair_slot]  191 us
    gather x2, local copies, waits for them, and re-layouts, device_step(): send_buf = hidden[slot_token].reshape(n_local, owners, capacity, d_model)  132 us
    reduce_sum x2, other arithmetic, combine(): jnp.sum(gate_probs[..., None] * pair_out.astype(jnp.float32), axis=-2)  113 us
  transfers between devices with their start and end apart: 10, of which 4 were waited for; matrix products, arithmetic and copies ran while one was open for 48% of the time, Pallas kernels for 0%

commit v1 on v0

v1 whole, which is shorter than its diff:
```python
import jax
import jax.numpy as jnp
from jax import lax
from jax.experimental import pallas as pl
from jax.experimental.pallas import tpu as pltpu
from jax.sharding import PartitionSpec as P


NORM_EPS = 1e-5
ROW_TILE = 256
COL_CHUNK = 256
OUT_TILE = 1024
MIX_TILE = 256


def rms_norm(stream, norm_row):
    widened = stream.astype(jnp.float32)
    inv_rms = lax.rsqrt(jnp.mean(widened * widened, axis=-1, keepdims=True) + NORM_EPS)
    return (widened * inv_rms * norm_row).astype(jnp.bfloat16)


def block_order(routes_l, experts):
    tok_dev = routes_l.shape[0]
    ids = jnp.arange(experts, dtype=jnp.int32)
    chosen = (routes_l[:, 0:1] == ids) | (routes_l[:, 1:2] == ids)
    counts = jnp.sum(chosen.astype(jnp.int32), axis=0)
    common = jnp.sum(jnp.where(counts == tok_dev, ids, 0))
    second = routes_l[:, 0] + routes_l[:, 1] - common
    key = second * tok_dev + jnp.arange(tok_dev, dtype=jnp.int32)
    place = jnp.sum((key[:, None] < key[None, :]).astype(jnp.int32), axis=0)
    start = jnp.sum((second[:, None] < ids).astype(jnp.int32), axis=0)
    stop = jnp.sum((second[:, None] <= ids).astype(jnp.int32), axis=0)
    start = jnp.where(ids == common, 0, start)
    stop = jnp.where(ids == common, tok_dev, stop)
    return place, start, stop


def at_place(place, values):
    slots = jnp.arange(place.shape[0], dtype=jnp.int32)
    return jnp.sum(jnp.where(place[:, None] == slots[None, :], values[:, None], 0), axis=0)


def tile_of(step, span):
    return jnp.minimum(span[0] + step, span[1])


def inner_rows(after, span, rows, gates, ups):
    tok, d_model = rows.shape
    part = gates[0][0].shape[-1]
    n_parts = len(gates)
    width = n_parts * part
    sources = list(gates) + list(ups)

    def kernel(span, after_ref, rows_ref, *refs):
        weight_refs, (act_ref, held, sems) = refs[:len(sources)], refs[len(sources):]
        i = pl.program_id(0)

        def copies(q):
            found = []
            for m in range(2):
                ref, lead = weight_refs[m * n_parts + q], sources[m * n_parts + q][1]
                found.append(pltpu.make_async_copy(ref.at[lead] if lead else ref, held.at[m, :, pl.ds(q * part, part)], sems.at[m, q]))
            return found

        @pl.when(i == 0)
        def _():
            for q in range(n_parts):
                for copy in copies(q):
                    copy.start()

        @pl.when(span[0] + i <= span[1])
        def _():
            rows = rows_ref[...]
            ready = 0
            for first in range(0, width, COL_CHUNK):
                cols = slice(first, first + COL_CHUNK)
                while ready * part < first + COL_CHUNK and ready < n_parts:
                    @pl.when(i == 0)
                    def _():
                        for copy in copies(ready):
                            copy.wait()

                    ready += 1
                pre_gate = jnp.dot(rows, held[0, :, cols], preferred_element_type=jnp.float32)
                pre_up = jnp.dot(rows, held[1, :, cols], preferred_element_type=jnp.float32)
                act_ref[:, cols] = (jax.nn.silu(pre_gate) * pre_up).astype(jnp.bfloat16)

    return pl.pallas_call(
        kernel,
        out_shape=jax.ShapeDtypeStruct((tok, width), jnp.bfloat16),
        grid_spec=pltpu.PrefetchScalarGridSpec(
            num_scalar_prefetch=1, grid=(tok // ROW_TILE,),
            in_specs=[pl.BlockSpec(memory_space=pl.ANY), pl.BlockSpec((ROW_TILE, d_model), lambda i, s: (tile_of(i, s), 0))]
            + [pl.BlockSpec(memory_space=pl.ANY)] * len(sources),
            out_specs=pl.BlockSpec((ROW_TILE, width), lambda i, s: (tile_of(i, s), 0)),
            scratch_shapes=[pltpu.VMEM((2, d_model, width), jnp.bfloat16), pltpu.SemaphoreType.DMA((2, n_parts))]),
        compiler_params=pltpu.CompilerParams(dimension_semantics=("arbitrary",)),
        cost_estimate=pl.CostEstimate(flops=2 * tok * d_model * width, bytes_accessed=4 * d_model * width, transcendentals=0),
        name="inner_rows",
    )(span, after, rows, *[s[0] for s in sources])


def outer_rows(after, span, acts, downs):
    tok = acts[0].shape[0]
    part = acts[0].shape[1] * len(acts) // len(downs)
    cols = sum(piece[3] for piece in downs[0])
    tile = min(OUT_TILE, cols)
    flat, moves = [], [[] for _ in range(cols // tile)]
    for q, pieces in enumerate(downs):
        at = 0
        for array, lead, first, count in pieces:
            done = 0
            while done < count:
                size = min(count - done, tile - at % tile)
                moves[at // tile].append((len(flat), lead, first + done, q * part, at % tile, size))
                at, done = at + size, done + size
            flat.append(array)
    most = max(len(m) for m in moves)

    def kernel(span, after_ref, *refs):
        act_refs, down_refs = refs[:len(acts)], refs[len(acts):len(acts) + len(flat)]
        out_ref, held, sems = refs[len(acts) + len(flat):]
        c, i = pl.program_id(0), pl.program_id(1)

        def copies(n):
            return [pltpu.make_async_copy(down_refs[a].at[lead + (slice(None), pl.ds(first, size))],
                                          held.at[n, pl.ds(row, part), pl.ds(col, size)], sems.at[n, j])
                    for j, (a, lead, first, row, col, size) in enumerate(moves[n])]

        @pl.when((c == 0) & (i == 0))
        def _():
            for n in range(len(moves)):
                for copy in copies(n):
                    copy.start()

        for n in range(len(moves)):
            @pl.when((c == n) & (i == 0))
            def _():
                for copy in copies(n):
                    copy.wait()

        @pl.when(span[0] + i <= span[1])
        def _():
            total, at = None, 0
            for act in act_refs:
                depth = act.shape[1]
                term = jnp.dot(act[...], held[c, at:at + depth], preferred_element_type=jnp.float32)
                total = term if total is None else total + term
                at += depth
            out_ref[...] = total.astype(jnp.bfloat16)

    return pl.pallas_call(
        kernel,
        out_shape=jax.ShapeDtypeStruct((tok, cols), jnp.bfloat16),
        grid_spec=pltpu.PrefetchScalarGridSpec(
            num_scalar_prefetch=1, grid=(cols // tile, tok // ROW_TILE),
            in_specs=[pl.BlockSpec(memory_space=pl.ANY)]
            + [pl.BlockSpec((ROW_TILE, a.shape[1]), lambda c, i, s: (tile_of(i, s), 0)) for a in acts]
            + [pl.BlockSpec(memory_space=pl.ANY)] * len(flat),
            out_specs=pl.BlockSpec((ROW_TILE, tile), lambda c, i, s: (tile_of(i, s), c)),
            scratch_shapes=[pltpu.VMEM((len(moves), part * len(downs), tile), jnp.bfloat16),
                            pltpu.SemaphoreType.DMA((len(moves), most))]),
        compiler_params=pltpu.CompilerParams(dimension_semantics=("arbitrary", "arbitrary")),
        cost_estimate=pl.CostEstimate(flops=tok * cols * part * len(downs), bytes_accessed=2 * len(downs) * cols * part,
                                      transcendentals=0),
        name="outer_rows",
    )(span, after, *acts, *flat)


def mix(ranges, stream, gates, parts):
    tok, d_model = stream.shape
    cuts = max(len(p) for p in parts)
    width = d_model // cuts

    def kernel(ranges, stream_ref, gates_ref, *refs):
        out_ref = refs[-1]
        row = lax.broadcasted_iota(jnp.int32, (MIX_TILE, 1), 0) + pl.program_id(0) * MIX_TILE
        for c in range(cuts):
            cols = slice(c * width, (c + 1) * width)
            mixed = jnp.zeros((MIX_TILE, width), jnp.float32)
            at = 0
            for e, pieces in enumerate(parts):
                ref = refs[at + c][...] if len(pieces) > 1 else refs[at][:, cols]
                at += len(pieces)
                picked = (row >= ranges[e]) & (row < ranges[len(parts) + e])
                mixed += jnp.where(picked, gates_ref[:, e:e + 1] * ref.astype(jnp.float32), 0.0)
            out_ref[:, cols] = (stream_ref[:, cols].astype(jnp.float32) + mixed).astype(jnp.bfloat16)

    flat = [p for pieces in parts for p in pieces]
    row_spec = lambda cols: pl.BlockSpec((MIX_TILE, cols), lambda i, s: (i, 0))
    return pl.pallas_call(
        kernel,
        out_shape=jax.ShapeDtypeStruct((tok, d_model), jnp.bfloat16),
        grid_spec=pltpu.PrefetchScalarGridSpec(
            num_scalar_prefetch=1, grid=(tok // MIX_TILE,),
            in_specs=[row_spec(d_model), row_spec(gates.shape[1])] + [row_spec(p.shape[1]) for p in flat],
            out_specs=row_spec(d_model)),
        compiler_params=pltpu.CompilerParams(dimension_semantics=("arbitrary",)),
        cost_estimate=pl.CostEstimate(flops=20 * tok * d_model, bytes_accessed=12 * tok * d_model, transcendentals=0),
        name="mix",
    )(ranges, stream, gates, *flat)


CUTS = ((1, 4), (1, 4))


def solution(mesh):
    owners, shards = mesh.shape["ep"], mesh.shape["fsdp"]
    token_spec = P(("rep", "ep", "fsdp"), None)
    expert_in_spec = P(None, "ep", None, "fsdp")
    expert_out_spec = P(None, "ep", "fsdp", None)
    route_spec = P(None, ("rep", "ep", "fsdp"), None)
    swap = [(i, owners - 1 - i) for i in range(owners)]

    def device_step(x_in, norm_w, router_w, gate_w, up_w, down_w, routes):
        layers, tok_dev, _ = routes.shape
        experts = router_w.shape[2]
        n_local = gate_w.shape[1]
        d_model = x_in.shape[1]
        mine = lax.axis_index("ep")

        def across(v):
            return lax.ppermute(v, "fsdp", [(i, (i + shards // 2) % shards) for i in range(shards)])

        def beside(v):
            return lax.ppermute(v, "fsdp", [(i, i ^ 1) for i in range(shards)])

        near = []
        for param in (gate_w, up_w, down_w):
            near.append(beside(param))
        far = [[None] * n_local for _ in range(layers)]
        for layer in range(layers):
            for k in range(n_local):
                cuts = CUTS[layer][k]
                width = d_model // cuts
                pieces = [gate_w[layer, k], up_w[layer, k]]
                pieces += [down_w[layer, k][:, c * width:(c + 1) * width] for c in range(cuts)]
                out = []
                for piece in pieces:
                    there = across(piece)
                    out.append((there, beside(there)))
                far[layer][k] = out

        orders = [block_order(routes[layer], experts) for layer in range(layers)]
        bounds = jnp.stack([jnp.stack(o[1:]) for o in orders])
        peer_bounds = lax.ppermute(bounds, "ep", swap)
        tokens = jnp.arange(tok_dev, dtype=jnp.int32)

        def spans(table, layer):
            start, stop = table[layer, 0], table[layer, 1]
            both = jnp.stack([start // ROW_TILE, (stop - 1) // ROW_TILE], axis=1)
            return [jnp.where(mine == 0, both[k], both[n_local + k]) for k in range(n_local)]

        def own_first(table):
            return jnp.where(mine == 0, table, jnp.roll(table, n_local, axis=-1))

        stream = x_in
        for layer in range(layers):
            place = orders[layer][0]
            if layer == 0:
                index = at_place(place, tokens)
            else:
                index = at_place(place, orders[layer - 1][0])
            stream = stream[index]
            hidden = rms_norm(stream, norm_w[layer])
            peer_hidden = lax.ppermute(hidden, "ep", swap)
            logits = own_first(jnp.dot(hidden, router_w[layer], preferred_element_type=jnp.float32))
            ranges = own_first(bounds[layer])
            row = tokens[:, None]
            picked = (row >= ranges[0]) & (row < ranges[1])
            top = jnp.max(jnp.where(picked, logits, -jnp.inf), axis=-1, keepdims=True)
            weight = jnp.where(picked, jnp.exp(jnp.where(picked, logits - top, 0.0)), 0.0)
            gates = weight / jnp.sum(weight, axis=-1, keepdims=True)

            own_spans, peer_spans = spans(bounds, layer), spans(peer_bounds, layer)

            def close(after, k, span, rows):
                return inner_rows(after, span, rows, [(gate_w, (layer, k)), (near[0], (layer, k))],
                                  [(up_w, (layer, k)), (near[1], (layer, k))])

            def distant(after, k, span, rows):
                pair = far[layer][k]
                return inner_rows(after, span, rows, [(v, ()) for v in pair[0]], [(v, ()) for v in pair[1]])

            def outer(after, k, span, acts, pieces):
                cols = far[layer][k][2][0].shape[1]
                first, count = pieces[0] * cols, len(pieces) * cols
                return outer_rows(after, span, acts, [[(down_w, (layer, k), first, count)], [(near[2], (layer, k), first, count)]]
                                  + [[(far[layer][k][2 + c][side], (), 0, cols) for c in pieces] for side in range(2)])

            def step(make, *args):
                made = make(*args)
                return made

            def send_back(made):
                return lax.ppermute(made, "ep", swap)

            own_close, peer_close = [hidden], [None]
            for k in range(n_local):
                own_close.append(step(close, own_close[-1], k, own_spans[k], hidden))
            own_far = step(distant, own_close[-1], 0, own_spans[0], hidden)
            peer_close[0] = own_far
            for k in range(n_local):
                peer_close.append(step(close, peer_close[-1], k, peer_spans[k], peer_hidden))
            own_parts, back_parts, last = [], [], peer_close[-1]
            for k in range(n_local):
                every = list(range(CUTS[layer][k]))
                last = peer_far = step(distant, last, k, peer_spans[k], peer_hidden)
                back = []
                for c in every:
                    last = step(outer, last, k, peer_spans[k], [peer_close[1 + k], peer_far], [c])
                    back.append(send_back(last))
                if k > 0:
                    last = own_far = step(distant, last, k, own_spans[k], hidden)
                last = step(outer, last, k, own_spans[k], [own_close[1 + k], own_far], every)
                own_parts.append([last])
                back_parts.append(back)
            stream = mix(ranges.reshape(-1), stream, gates, own_parts + back_parts)
        return stream[orders[layers - 1][0]]

    return jax.shard_map(device_step, mesh=mesh,
                         in_specs=(token_spec, P(), P(), expert_in_spec, expert_in_spec, expert_out_spec, route_spec),
                         out_specs=token_spec, check_vma=False)
```

time: 3630 us -> 2430 us (0.67)
  matrix products: 1290 us -> 11.3 us
  Pallas kernels: 0 us -> 974 us
  local copies, waits for them, and re-layouts: 749 us -> 127 us
  waiting for transfers between devices: 1340 us -> 868 us
  starting transfers between devices: 52.9 us -> 391 us
  other arithmetic: 167 us -> 53.8 us
    all_to_all x4 -> x0, waiting for transfers between devices: 1330 us -> none  [the longest x2 724 us: device_step(): recv_buf = lax.all_to_all(send_buf, 'ep', 1, 1, tiled=True)]
    dot_general x8 -> x2, matrix products: 1290 us -> 11.3 us  [device_step(): jnp.dot(hidden, router_w[layer], preferred_element_type=jnp.float32)]
    pallas_call x0 -> x32, Pallas kernels: none -> 974 us  [the longest x16 590 us: inner_rows(): pl.pallas_call(kernel, out_shape=jax.ShapeDtypeStruct((tok, width), jnp.b...]
    ppermute x0 -> x52, waiting for transfers between devices: none -> 868 us  [the longest x18 550 us: across(): lax.ppermute(v, 'fsdp', [(i, (i + shards // 2) % shards) for i in range(s...]
    ppermute x0 -> x52, starting transfers between devices: none -> 391 us  [the longest x21 214 us: beside(): return lax.ppermute(v, 'fsdp', [(i, i ^ 1) for i in range(shards)])]
    gather x10 -> x3, local copies, waits for them, and re-layouts: 396 us -> 63.2 us  [the longest x2 42.4 us: device_step(): stream = stream[index]]
    reduce_sum x6 -> x11, other arithmetic: 114 us -> 13.3 us  [the longest x1 6.13 us: at_place(): jnp.sum(jnp.where(place[:, None] == slots[None, :], values[:, None], 0),...]
    all_to_all x4 -> x0, local copies, waits for them, and re-layouts: 96.6 us -> none  [the longest x2 50.9 us: device_step(): recv_buf = lax.all_to_all(send_buf, 'ep', 1, 1, tiled=True)]
  transfers between devices with their start and end apart: 10 -> 52, of which waited for: 4 -> 12; matrix products, arithmetic and copies ran while one was open for 48% -> 7% of each run, Pallas kernels for 0% -> 39%
where the time goes in v1:
time: 2430 us
  Pallas kernels  974 us (40%)
  waiting for transfers between devices  868 us (36%)
  starting transfers between devices  391 us (16%)
  local copies, waits for them, and re-layouts  127 us (5%)
  other arithmetic  53.8 us (2%)
    pallas_call x16, Pallas kernels, inner_rows(): pl.pallas_call(kernel, out_shape=jax.ShapeDtypeStruct((tok, width), jnp.b...  590 us
    ppermute x18, waiting for transfers between devices, across(): lax.ppermute(v, 'fsdp', [(i, (i + shards // 2) % shards) for i in range(s...  550 us
    pallas_call x14, Pallas kernels, outer_rows(): pl.pallas_call(kernel, out_shape=jax.ShapeDtypeStruct((tok, cols), jnp.bf...  340 us
    ppermute x10, waiting for transfers between devices, send_back(): return lax.ppermute(made, 'ep', swap)  317 us
    ppermute x21, starting transfers between devices, beside(): return lax.ppermute(v, 'fsdp', [(i, i ^ 1) for i in range(shards)])  214 us
    ppermute x18, starting transfers between devices, across(): lax.ppermute(v, 'fsdp', [(i, (i + shards // 2) % shards) for i in range(s...  169 us
  transfers between devices with their start and end apart: 52, of which 12 were waited for; matrix products, arithmetic and copies ran while one was open for 7% of the time, Pallas kernels for 39%

profile of v1, /device:TPU:0, one launch (start us, length us, event | category | flops | bytes accessed | tf_op | source)
XLA Modules:
  0.0 2425.4 jit_solution(4041054100333166295)
XLA Ops:
  0.8 17.1 slice_bitcast_fusion.2
  21.0 17.0 slice_bitcast_fusion.1
  56.7 21.2 gather_fusion
  98.0 48.4 %collective-permute-done.3.refs_0_ = bf16[2048,1408]{1,0:T(8,128)(2,1)} collective-permute-done((bf16[2048,1408]{1,0:T(8,128)(2,1)}, bf16[2048,1408]{1,0:T(8,128)(2,1)}, u32[]{:S(2)}, u32[]{:S(2)}) %collective-permute-start.3) | collective-permute-done | bytes 5767200 | tf_op jit(solution)/shard_map/ppermute | solution.py:223
  149.1 120.2 %collective-permute-done.5.refs_2_ = bf16[2048,1408]{1,0:T(8,128)(2,1)} collective-permute-done((bf16[2048,1408]{1,0:T(8,128)(2,1)}, bf16[2048,1408]{1,0:T(8,128)(2,1)}, u32[]{:S(2)}, u32[]{:S(2)}) %collective-permute-start.5) | collective-permute-done | bytes 5767200 | tf_op jit(solution)/shard_map/ppermute | solution.py:223
  272.2 15.7 slice_bitcast_fusion
  304.9 14.6 inner_rows.16.after_ref.refs_0_
  319.5 59.0 %inner_rows.17.after_ref.refs_0_ = bf16[2048,2816]{1,0:T(8,128)(2,1)} custom-call(s32[2]{0:T(128)} %get-tuple-element.15.span, bf16[2048,2816]{1,0:T(8,128)(2,1)} %inner_rows.16.after_ref.refs_0_, bf16[2048,2048]{1,0:T(8,128)(2,1)} %fusion.2.after_ref.rows_ref, bf16[2,2,2048,1408]{3,2,1,0:T(8,128)(2,1)} %refs_0_.15, ...), custom_call_target="tpu_custom_call" | custom-call | flops 23622320128 | bytes 23068672 | tf_op jit(solution)/shard_map/inner_rows/pallas_call | solution.py:88
  378.5 14.6 inner_rows.18.after_ref.refs_1_
  393.1 35.7 %collective-permute-done.9.refs_4_ = bf16[1408,2048]{1,0:T(8,128)(2,1)} collective-permute-done((bf16[1408,2048]{1,0:T(8,128)(2,1)}, bf16[1408,2048]{1,0:T(8,128)(2,1)}, u32[]{:S(2)}, u32[]{:S(2)}) %collective-permute-start.9) | collective-permute-done | bytes 5767200 | tf_op jit(solution)/shard_map/ppermute | solution.py:223
  428.8 28.5 %collective-permute-start.15 = (bf16[1408,512]{1,0:T(8,128)(2,1)S(1)}, bf16[1408,512]{1,0:T(8,128)(2,1)S(1)}, u32[]{:S(2)}, u32[]{:S(2)}) collective-permute-start(bf16[1408,512]{1,0:T(8,128)(2,1)S(1)} %get-tuple-element.46), channel_id=1, source_target_pairs={{0,2},{1,3},{2,0},{3,1},{4,6},{5,7},{6,4},{7,5}} | collective-permute-start | bytes 4325384 | tf_op jit(solution)/shard_map/ppermute | solution.py:223
  457.3 95.1 %collective-permute-done.11.refs_0_ = bf16[2048,1408]{1,0:T(8,128)(2,1)} collective-permute-done((bf16[2048,1408]{1,0:T(8,128)(2,1)}, bf16[2048,1408]{1,0:T(8,128)(2,1)}, u32[]{:S(2)}, u32[]{:S(2)}) %collective-permute-start.11) | collective-permute-done | bytes 5767200 | tf_op jit(solution)/shard_map/ppermute | solution.py:223
  552.4 123.6 %collective-permute-done.13.refs_2_ = bf16[2048,1408]{1,0:T(8,128)(2,1)} collective-permute-done((bf16[2048,1408]{1,0:T(8,128)(2,1)}, bf16[2048,1408]{1,0:T(8,128)(2,1)}, u32[]{:S(2)}, u32[]{:S(2)}) %collective-permute-start.13) | collective-permute-done | bytes 5767200 | tf_op jit(solution)/shard_map/ppermute | solution.py:223
  690.9 59.4 %inner_rows.20.after_ref.refs_0_ = bf16[2048,2816]{1,0:T(8,128)(2,1)} custom-call(s32[2]{0:T(128)} %get-tuple-element.17.span, bf16[2048,2816]{1,0:T(8,128)(2,1)} %inner_rows.19.after_ref.refs_0_, bf16[2048,2048]{1,0:T(8,128)(2,1)} %collective-permute-done.7.rows_ref, bf16[2,2,2048,1408]{3,2,1,0:T(8,128)(2,1)} %refs_0_.15, ...), custom_call_target="tpu_custom_call" | custom-call | flops 23622320128 | bytes 23068672 | tf_op jit(solution)/shard_map/inner_rows/pallas_call | solution.py:88
  768.3 15.2 outer_rows.14.after_ref
  799.5 93.6 %collective-permute-start.16 = (bf16[1408,512]{1,0:T(8,128)(2,1)S(1)}, bf16[1408,512]{1,0:T(8,128)(2,1)}, u32[]{:S(2)}, u32[]{:S(2)}) collective-permute-start(bf16[1408,512]{1,0:T(8,128)(2,1)S(1)} %collective-permute-done.15.refs_4_), channel_id=1, source_target_pairs={{0,1},{1,0},{2,3},{3,2},{4,5},{5,4},{6,7},{7,6}} | collective-permute-start | bytes 4325384 | tf_op jit(solution)/shard_map/ppermute | solution.py:226
  893.2 15.3 outer_rows.15.after_ref.refs_0_
  922.5 19.6 collective-permute-start.30
  942.1 84.6 %collective-permute-start.18 = (bf16[1408,512]{1,0:T(8,128)(2,1)S(1)}, bf16[1408,512]{1,0:T(8,128)(2,1)S(1)}, u32[]{:S(2)}, u32[]{:S(2)}) collective-permute-start(bf16[1408,512]{1,0:T(8,128)(2,1)S(1)} %collective-permute-done.17.refs_4_.refs_5_), channel_id=1, source_target_pairs={{0,1},{1,0},{2,3},{3,2},{4,5},{5,4},{6,7},{7,6}} | collective-permute-start | bytes 4325384 | tf_op jit(solution)/shard_map/ppermute | solution.py:226
  1026.7 58.9 %inner_rows.22.after_ref.refs_1_ = bf16[2048,2816]{1,0:T(8,128)(2,1)} custom-call(s32[2]{0:T(128)} %get-tuple-element.17.span, bf16[2048,2048]{1,0:T(8,128)(2,1)} %outer_rows.15.after_ref.refs_0_, bf16[2048,2048]{1,0:T(8,128)(2,1)} %collective-permute-done.7.rows_ref, bf16[2048,1408]{1,0:T(8,128)(2,1)} %collective-permute-done.11.refs_0_, ...), custom_call_target="tpu_custom_call" | custom-call | flops 23622320128 | bytes 23068672 | tf_op jit(solution)/shard_map/inner_rows/pallas_call | solution.py:88
  1086.1 20.2 outer_rows.16.after_ref
  1106.5 20.2 outer_rows.17.after_ref
  1126.7 20.2 outer_rows.18.after_ref
  1148.1 20.2 outer_rows.19.after_ref
  1168.4 59.3 %inner_rows.23.after_ref.refs_1_ = bf16[2048,2816]{1,0:T(8,128)(2,1)} custom-call(s32[2]{0:T(128)} %get-tuple-element.15.span, bf16[2048,512]{1,0:T(8,128)(2,1)} %outer_rows.19.after_ref, bf16[2048,2048]{1,0:T(8,128)(2,1)} %fusion.2.after_ref.rows_ref, bf16[2048,1408]{1,0:T(8,128)(2,1)} %collective-permute-done.11.refs_0_, ...), custom_call_target="tpu_custom_call" | custom-call | flops 23622320128 | bytes 23068672 | tf_op jit(solution)/shard_map/inner_rows/pallas_call | solution.py:88
  1227.7 72.5 %collective-permute-done.27.refs_6_ = bf16[2048,512]{1,0:T(8,128)(2,1)} collective-permute-done((bf16[2048,512]{1,0:T(8,128)(2,1)}, bf16[2048,512]{1,0:T(8,128)(2,1)}, u32[]{:S(2)}, u32[]{:S(2)}) %collective-permute-start.27) | collective-permute-done | bytes 2097184 | tf_op jit(solution)/shard_map/ppermute | solution.py:296
  1300.2 59.2 %outer_rows.20.refs_1_ = bf16[2048,2048]{1,0:T(8,128)(2,1)} custom-call(s32[2]{0:T(128)} %get-tuple-element.15.span, bf16[2048,2816]{1,0:T(8,128)(2,1)} %inner_rows.23.after_ref.refs_1_, bf16[2048,2816]{1,0:T(8,128)(2,1)} %inner_rows.17.after_ref.refs_0_, bf16[2048,2816]{1,0:T(8,128)(2,1)} %inner_rows.23.after_ref.refs_1_, ...), custom_call_target="tpu_custom_call" | custom-call | flops 23622320128 | bytes 23068672 | tf_op jit(solution)/shard_map/outer_rows/pallas_call | solution.py:152
  1361.5 28.1 %collective-permute-done.24.refs_3_ = bf16[2048,512]{1,0:T(8,128)(2,1)} collective-permute-done((bf16[2048,512]{1,0:T(8,128)(2,1)S(1)}, bf16[2048,512]{1,0:T(8,128)(2,1)}, u32[]{:S(2)}, u32[]{:S(2)}) %collective-permute-start.24) | collective-permute-done | bytes 2097184 | tf_op jit(solution)/shard_map/ppermute | solution.py:296
  1389.6 22.0 mix.2
  1411.6 21.2 gather_fusion.1
  1452.5 59.1 %inner_rows.24.after_ref.refs_0_ = bf16[2048,2816]{1,0:T(8,128)(2,1)} custom-call(s32[2]{0:T(128)} %get-tuple-element.12.span, bf16[2048,2048]{1,0:T(8,128)(2,1)} %fusion.5.after_ref.rows_ref, bf16[2048,2048]{1,0:T(8,128)(2,1)} %fusion.5.after_ref.rows_ref, bf16[2,2,2048,1408]{3,2,1,0:T(8,128)(2,1)} %refs_0_.15, ...), custom_call_target="tpu_custom_call" | custom-call | flops 23622320128 | bytes 23068672 | tf_op jit(solution)/shard_map/inner_rows/pallas_call | solution.py:88
  1515.3 46.4 %inner_rows.25.after_ref.refs_0_ = bf16[2048,2816]{1,0:T(8,128)(2,1)} custom-call(s32[2]{0:T(128)} %get-tuple-element.11.span, bf16[2048,2816]{1,0:T(8,128)(2,1)} %inner_rows.24.after_ref.refs_0_, bf16[2048,2048]{1,0:T(8,128)(2,1)} %fusion.5.after_ref.rows_ref, bf16[2,2,2048,1408]{3,2,1,0:T(8,128)(2,1)} %refs_0_.15, ...), custom_call_target="tpu_custom_call" | custom-call | flops 23622320128 | bytes 23068672 | tf_op jit(solution)/shard_map/inner_rows/pallas_call | solution.py:88
  1561.7 59.0 %inner_rows.26.after_ref.refs_1_ = bf16[2048,2816]{1,0:T(8,128)(2,1)} custom-call(s32[2]{0:T(128)} %get-tuple-element.12.span, bf16[2048,2816]{1,0:T(8,128)(2,1)} %inner_rows.25.after_ref.refs_0_, bf16[2048,2048]{1,0:T(8,128)(2,1)} %fusion.5.after_ref.rows_ref, bf16[2048,1408]{1,0:T(8,128)(2,1)} %collective-permute-done.28.refs_0_, ...), custom_call_target="tpu_custom_call" | custom-call | flops 23622320128 | bytes 23068672 | tf_op jit(solution)/shard_map/inner_rows/pallas_call | solution.py:88
  1620.8 14.5 collective-permute-start.34
  1635.2 98.9 %collective-permute-done.37.refs_2_ = bf16[2048,1408]{1,0:T(8,128)(2,1)} collective-permute-done((bf16[2048,1408]{1,0:T(8,128)(2,1)}, bf16[2048,1408]{1,0:T(8,128)(2,1)}, u32[]{:S(2)}, u32[]{:S(2)}) %collective-permute-start.37) | collective-permute-done | bytes 5767200 | tf_op jit(solution)/shard_map/ppermute | solution.py:223
  1734.7 27.3 %inner_rows.27.after_ref.refs_0_ = bf16[2048,2816]{1,0:T(8,128)(2,1)} custom-call(s32[2]{0:T(128)} %get-tuple-element.14.span, bf16[2048,2816]{1,0:T(8,128)(2,1)} %inner_rows.26.after_ref.refs_1_, bf16[2048,2048]{1,0:T(8,128)(2,1)} %collective-permute-done.32.rows_ref, bf16[2,2,2048,1408]{3,2,1,0:T(8,128)(2,1)} %refs_0_.15, ...), custom_call_target="tpu_custom_call" | custom-call | flops 23622320128 | bytes 23068672 | tf_op jit(solution)/shard_map/inner_rows/pallas_call | solution.py:88
  1776.5 27.4 %inner_rows.29.after_ref.refs_1_ = bf16[2048,2816]{1,0:T(8,128)(2,1)} custom-call(s32[2]{0:T(128)} %get-tuple-element.14.span, bf16[2048,2816]{1,0:T(8,128)(2,1)} %inner_rows.28.after_ref.refs_0_, bf16[2048,2048]{1,0:T(8,128)(2,1)} %collective-permute-done.32.rows_ref, bf16[2048,1408]{1,0:T(8,128)(2,1)} %collective-permute-done.28.refs_0_, ...), custom_call_target="tpu_custom_call" | custom-call | flops 23622320128 | bytes 23068672 | tf_op jit(solution)/shard_map/inner_rows/pallas_call | solution.py:88
  1803.9 77.4 %collective-permute-start.43 = (bf16[1408,512]{1,0:T(8,128)(2,1)}, bf16[1408,512]{1,0:T(8,128)(2,1)}, u32[]{:S(2)}, u32[]{:S(2)}) collective-permute-start(bf16[1408,512]{1,0:T(8,128)(2,1)} %get-tuple-element.40), channel_id=1, source_target_pairs={{0,2},{1,3},{2,0},{3,1},{4,6},{5,7},{6,4},{7,5}} | collective-permute-start | bytes 4325384 | tf_op jit(solution)/shard_map/ppermute | solution.py:223
  1881.3 29.7 %outer_rows.21.after_ref = bf16[2048,2048]{1,0:T(8,128)(2,1)} custom-call(s32[2]{0:T(128)} %get-tuple-element.14.span, bf16[2048,2816]{1,0:T(8,128)(2,1)} %inner_rows.29.after_ref.refs_1_, bf16[2048,2816]{1,0:T(8,128)(2,1)} %inner_rows.27.after_ref.refs_0_, bf16[2048,2816]{1,0:T(8,128)(2,1)} %inner_rows.29.after_ref.refs_1_, ...), custom_call_target="tpu_custom_call" | custom-call | flops 23622320128 | bytes 23068672 | tf_op jit(solution)/shard_map/outer_rows/pallas_call | solution.py:152
  1911.1 29.3 %collective-permute-start.45 = (bf16[1408,512]{1,0:T(8,128)(2,1)}, bf16[1408,512]{1,0:T(8,128)(2,1)}, u32[]{:S(2)}, u32[]{:S(2)}) collective-permute-start(bf16[1408,512]{1,0:T(8,128)(2,1)} %get-tuple-element.39), channel_id=1, source_target_pairs={{0,2},{1,3},{2,0},{3,1},{4,6},{5,7},{6,4},{7,5}} | collective-permute-start | bytes 4325384 | tf_op jit(solution)/shard_map/ppermute | solution.py:223
  1940.4 59.0 %outer_rows.22.after_ref.refs_0_ = bf16[2048,2048]{1,0:T(8,128)(2,1)} custom-call(s32[2]{0:T(128)} %get-tuple-element.12.span, bf16[2048,2048]{1,0:T(8,128)(2,1)} %outer_rows.21.after_ref, bf16[2048,2816]{1,0:T(8,128)(2,1)} %inner_rows.24.after_ref.refs_0_, bf16[2048,2816]{1,0:T(8,128)(2,1)} %inner_rows.26.after_ref.refs_1_, ...), custom_call_target="tpu_custom_call" | custom-call | flops 23622320128 | bytes 23068672 | tf_op jit(solution)/shard_map/outer_rows/pallas_call | solution.py:152
  1999.5 18.0 collective-permute-start.40
  2018.1 14.9 inner_rows.30.after_ref.refs_1_
  2069.3 46.4 %inner_rows.31.after_ref.refs_1_ = bf16[2048,2816]{1,0:T(8,128)(2,1)} custom-call(s32[2]{0:T(128)} %get-tuple-element.11.span, bf16[2048,512]{1,0:T(8,128)(2,1)} %outer_rows.26.after_ref, bf16[2048,2048]{1,0:T(8,128)(2,1)} %fusion.5.after_ref.rows_ref, bf16[2048,1408]{1,0:T(8,128)(2,1)} %collective-permute-done.35.refs_0_, ...), custom_call_target="tpu_custom_call" | custom-call | flops 23622320128 | bytes 23068672 | tf_op jit(solution)/shard_map/inner_rows/pallas_call | solution.py:88
  2115.7 48.6 %outer_rows.27.refs_1_ = bf16[2048,2048]{1,0:T(8,128)(2,1)} custom-call(s32[2]{0:T(128)} %get-tuple-element.11.span, bf16[2048,2816]{1,0:T(8,128)(2,1)} %inner_rows.31.after_ref.refs_1_, bf16[2048,2816]{1,0:T(8,128)(2,1)} %inner_rows.25.after_ref.refs_0_, bf16[2048,2816]{1,0:T(8,128)(2,1)} %inner_rows.31.after_ref.refs_1_, ...), custom_call_target="tpu_custom_call" | custom-call | flops 23622320128 | bytes 23068672 | tf_op jit(solution)/shard_map/outer_rows/pallas_call | solution.py:152
  2164.3 216.7 %collective-permute-done.51.refs_6_ = bf16[2048,512]{1,0:T(8,128)(2,1)} collective-permute-done((bf16[2048,512]{1,0:T(8,128)(2,1)}, bf16[2048,512]{1,0:T(8,128)(2,1)}, u32[]{:S(2)}, u32[]{:S(2)}) %collective-permute-start.51) | collective-permute-done | bytes 2097184 | tf_op jit(solution)/shard_map/ppermute | solution.py:296
  2382.3 22.0 mix.3
  2404.4 20.8 gather_fusion.2
  (200 shorter events, 208.2 us)
Async XLA Ops:
  0.0 302.8 %collective-permute-start.1 = (bf16[2,2,2048,1408]{3,2,1,0:T(8,128)(2,1)}, bf16[2,2,2048,1408]{3,2,1,0:T(8,128)(2,1)}, u32[]{:S(2)}, u32[]{:S(2)}) collective-permute-start(bf16[2,2,2048,1408]{3,2,1,0:T(8,128)(2,1)} %refs_0_.15), channel_id=1, source_target_pairs={{0,1},{1,0},{2,3},{3,2},{4,5},{5,4},{6,7},{7,6}} | collective-permute-start | bytes 69206024 | tf_op jit(solution)/shard_map/ppermute | solution.py:226
  0.8 302.5 %collective-permute-start.2 = (bf16[2,2,2048,1408]{3,2,1,0:T(8,128)(2,1)}, bf16[2,2,2048,1408]{3,2,1,0:T(8,128)(2,1)}, u32[]{:S(2)}, u32[]{:S(2)}) collective-permute-start(bf16[2,2,2048,1408]{3,2,1,0:T(8,128)(2,1)} %refs_2_.36), channel_id=1, source_target_pairs={{0,1},{1,0},{2,3},{3,2},{4,5},{5,4},{6,7},{7,6}} | collective-permute-start | bytes 69206024 | tf_op jit(solution)/shard_map/ppermute | solution.py:226
  18.0 128.4 %collective-permute-start.3 = (bf16[2048,1408]{1,0:T(8,128)(2,1)}, bf16[2048,1408]{1,0:T(8,128)(2,1)}, u32[]{:S(2)}, u32[]{:S(2)}) collective-permute-start(bf16[2048,1408]{1,0:T(8,128)(2,1)} %get-tuple-element.38), channel_id=1, source_target_pairs={{0,2},{1,3},{2,0},{3,1},{4,6},{5,7},{6,4},{7,5}} | collective-permute-start | bytes 17301512 | tf_op jit(solution)/shard_map/ppermute | solution.py:223
  38.0 231.4 %collective-permute-start.5 = (bf16[2048,1408]{1,0:T(8,128)(2,1)}, bf16[2048,1408]{1,0:T(8,128)(2,1)}, u32[]{:S(2)}, u32[]{:S(2)}) collective-permute-start(bf16[2048,1408]{1,0:T(8,128)(2,1)} %get-tuple-element.34), channel_id=1, source_target_pairs={{0,2},{1,3},{2,0},{3,1},{4,6},{5,7},{6,4},{7,5}} | collective-permute-start | bytes 17301512 | tf_op jit(solution)/shard_map/ppermute | solution.py:223
  43.9 39.8 %collective-permute-start = (s32[2,2,4]{2,1,0:T(2,128)S(1)}, s32[2,2,4]{2,1,0:T(2,128)S(1)}, u32[]{:S(2)}, u32[]{:S(2)}) collective-permute-start(s32[2,2,4]{2,1,0:T(2,128)S(1)} %pad_add_fusion), channel_id=1, source_target_pairs={{0,4},{4,0},{1,5},{5,1},{2,6},{6,2},{3,7},{7,3}} | collective-permute-start | bytes 200 | tf_op jit(solution)/shard_map/ppermute | solution.py:246
  83.6 683.1 %collective-permute-start.8 = (bf16[2,2,1408,2048]{3,2,1,0:T(8,128)(2,1)}, bf16[2,2,1408,2048]{3,2,1,0:T(8,128)(2,1)}, u32[]{:S(2)}, u32[]{:S(2)}) collective-permute-start(bf16[2,2,1408,2048]{3,2,1,0:T(8,128)(2,1)} %refs_2_.43), channel_id=1, source_target_pairs={{0,1},{1,0},{2,3},{3,2},{4,5},{5,4},{6,7},{7,6}} | collective-permute-start | bytes 69206024 | tf_op jit(solution)/shard_map/ppermute | solution.py:226
  146.4 143.8 %collective-permute-start.4 = (bf16[2048,1408]{1,0:T(8,128)(2,1)}, bf16[2048,1408]{1,0:T(8,128)(2,1)}, u32[]{:S(2)}, u32[]{:S(2)}) collective-permute-start(bf16[2048,1408]{1,0:T(8,128)(2,1)} %collective-permute-done.3.refs_0_), channel_id=1, source_target_pairs={{0,1},{1,0},{2,3},{3,2},{4,5},{5,4},{6,7},{7,6}} | collective-permute-start | bytes 17301512 | tf_op jit(solution)/shard_map/ppermute | solution.py:226
  290.2 385.8 %collective-permute-start.7 = (bf16[2048,2048]{1,0:T(8,128)(2,1)}, bf16[2048,2048]{1,0:T(8,128)(2,1)}, u32[]{:S(2)}, u32[]{:S(2)}) collective-permute-start(bf16[2048,2048]{1,0:T(8,128)(2,1)} %fusion.2.after_ref.rows_ref), channel_id=1, source_target_pairs={{0,4},{4,0},{1,5},{5,1},{2,6},{6,2},{3,7},{7,3}} | collective-permute-start | bytes 25165832 | tf_op jit(solution)/shard_map/ppermute | solution.py:266
  301.3 127.5 %collective-permute-start.9 = (bf16[1408,2048]{1,0:T(8,128)(2,1)}, bf16[1408,2048]{1,0:T(8,128)(2,1)}, u32[]{:S(2)}, u32[]{:S(2)}) collective-permute-start(bf16[1408,2048]{1,0:T(8,128)(2,1)} %get-tuple-element.30), channel_id=1, source_target_pairs={{0,2},{1,3},{2,0},{3,1},{4,6},{5,7},{6,4},{7,5}} | collective-permute-start | bytes 17301512 | tf_op jit(solution)/shard_map/ppermute | solution.py:223
  302.8 249.6 %collective-permute-start.11 = (bf16[2048,1408]{1,0:T(8,128)(2,1)}, bf16[2048,1408]{1,0:T(8,128)(2,1)}, u32[]{:S(2)}, u32[]{:S(2)}) collective-permute-start(bf16[2048,1408]{1,0:T(8,128)(2,1)} %get-tuple-element.37), channel_id=1, source_target_pairs={{0,2},{1,3},{2,0},{3,1},{4,6},{5,7},{6,4},{7,5}} | collective-permute-start | bytes 17301512 | tf_op jit(solution)/shard_map/ppermute | solution.py:223
  303.4 372.6 %collective-permute-start.13 = (bf16[2048,1408]{1,0:T(8,128)(2,1)}, bf16[2048,1408]{1,0:T(8,128)(2,1)}, u32[]{:S(2)}, u32[]{:S(2)}) collective-permute-start(bf16[2048,1408]{1,0:T(8,128)(2,1)} %get-tuple-element.33), channel_id=1, source_target_pairs={{0,2},{1,3},{2,0},{3,1},{4,6},{5,7},{6,4},{7,5}} | collective-permute-start | bytes 17301512 | tf_op jit(solution)/shard_map/ppermute | solution.py:223
  428.8 335.9 %collective-permute-start.15 = (bf16[1408,512]{1,0:T(8,128)(2,1)S(1)}, bf16[1408,512]{1,0:T(8,128)(2,1)S(1)}, u32[]{:S(2)}, u32[]{:S(2)}) collective-permute-start(bf16[1408,512]{1,0:T(8,128)(2,1)S(1)} %get-tuple-element.46), channel_id=1, source_target_pairs={{0,2},{1,3},{2,0},{3,1},{4,6},{5,7},{6,4},{7,5}} | collective-permute-start | bytes 4325384 | tf_op jit(solution)/shard_map/ppermute | solution.py:223
  552.4 213.8 %collective-permute-start.10 = (bf16[1408,2048]{1,0:T(8,128)(2,1)}, bf16[1408,2048]{1,0:T(8,128)(2,1)}, u32[]{:S(2)}, u32[]{:S(2)}) collective-permute-start(bf16[1408,2048]{1,0:T(8,128)(2,1)} %collective-permute-done.9.refs_4_), channel_id=1, source_target_pairs={{0,1},{1,0},{2,3},{3,2},{4,5},{5,4},{6,7},{7,6}} | collective-permute-start | bytes 17301512 | tf_op jit(solution)/shard_map/ppermute | solution.py:226
  676.0 350.7 %collective-permute-start.12 = (bf16[2048,1408]{1,0:T(8,128)(2,1)}, bf16[2048,1408]{1,0:T(8,128)(2,1)}, u32[]{:S(2)}, u32[]{:S(2)}) collective-permute-start(bf16[2048,1408]{1,0:T(8,128)(2,1)} %collective-permute-done.11.refs_0_), channel_id=1, source_target_pairs={{0,1},{1,0},{2,3},{3,2},{4,5},{5,4},{6,7},{7,6}} | collective-permute-start | bytes 17301512 | tf_op jit(solution)/shard_map/ppermute | solution.py:226
  676.0 350.7 %collective-permute-start.14 = (bf16[2048,1408]{1,0:T(8,128)(2,1)}, bf16[2048,1408]{1,0:T(8,128)(2,1)}, u32[]{:S(2)}, u32[]{:S(2)}) collective-permute-start(bf16[2048,1408]{1,0:T(8,128)(2,1)} %collective-permute-done.13.refs_2_), channel_id=1, source_target_pairs={{0,1},{1,0},{2,3},{3,2},{4,5},{5,4},{6,7},{7,6}} | collective-permute-start | bytes 17301512 | tf_op jit(solution)/shard_map/ppermute | solution.py:226
  766.8 339.6 %collective-permute-start.28 = (bf16[2048,1408]{1,0:T(8,128)(2,1)}, bf16[2048,1408]{1,0:T(8,128)(2,1)}, u32[]{:S(2)}, u32[]{:S(2)}) collective-permute-start(bf16[2048,1408]{1,0:T(8,128)(2,1)} %get-tuple-element.36), channel_id=1, source_target_pairs={{0,2},{1,3},{2,0},{3,1},{4,6},{5,7},{6,4},{7,5}} | collective-permute-start | bytes 17301512 | tf_op jit(solution)/shard_map/ppermute | solution.py:223
  784.0 138.5 %collective-permute-start.21 = (bf16[1408,512]{1,0:T(8,128)(2,1)}, bf16[1408,512]{1,0:T(8,128)(2,1)}, u32[]{:S(2)}, u32[]{:S(2)}) collective-permute-start(bf16[1408,512]{1,0:T(8,128)(2,1)} %get-tuple-element.43), channel_id=1, source_target_pairs={{0,2},{1,3},{2,0},{3,1},{4,6},{5,7},{6,4},{7,5}} | collective-permute-start | bytes 4325384 | tf_op jit(solution)/shard_map/ppermute | solution.py:223
  799.5 142.6 %collective-permute-start.16 = (bf16[1408,512]{1,0:T(8,128)(2,1)S(1)}, bf16[1408,512]{1,0:T(8,128)(2,1)}, u32[]{:S(2)}, u32[]{:S(2)}) collective-permute-start(bf16[1408,512]{1,0:T(8,128)(2,1)S(1)} %collective-permute-done.15.refs_4_), channel_id=1, source_target_pairs={{0,1},{1,0},{2,3},{3,2},{4,5},{5,4},{6,7},{7,6}} | collective-permute-start | bytes 4325384 | tf_op jit(solution)/shard_map/ppermute | solution.py:226
  922.5 305.2 %collective-permute-start.30 = (bf16[2048,1408]{1,0:T(8,128)(2,1)}, bf16[2048,1408]{1,0:T(8,128)(2,1)}, u32[]{:S(2)}, u32[]{:S(2)}) collective-permute-start(bf16[2048,1408]{1,0:T(8,128)(2,1)} %get-tuple-element.32), channel_id=1, source_target_pairs={{0,2},{1,3},{2,0},{3,1},{4,6},{5,7},{6,4},{7,5}} | collective-permute-start | bytes 17301512 | tf_op jit(solution)/shard_map/ppermute | solution.py:223
  942.1 143.6 %collective-permute-start.18 = (bf16[1408,512]{1,0:T(8,128)(2,1)S(1)}, bf16[1408,512]{1,0:T(8,128)(2,1)S(1)}, u32[]{:S(2)}, u32[]{:S(2)}) collective-permute-start(bf16[1408,512]{1,0:T(8,128)(2,1)S(1)} %collective-permute-done.17.refs_4_.refs_5_), channel_id=1, source_target_pairs={{0,1},{1,0},{2,3},{3,2},{4,5},{5,4},{6,7},{7,6}} | collective-permute-start | bytes 4325384 | tf_op jit(solution)/shard_map/ppermute | solution.py:226
  1026.7 100.0 %collective-permute-start.20 = (bf16[1408,512]{1,0:T(8,128)(2,1)}, bf16[1408,512]{1,0:T(8,128)(2,1)}, u32[]{:S(2)}, u32[]{:S(2)}) collective-permute-start(bf16[1408,512]{1,0:T(8,128)(2,1)} %collective-permute-done.19.refs_4_.refs_6_), channel_id=1, source_target_pairs={{0,1},{1,0},{2,3},{3,2},{4,5},{5,4},{6,7},{7,6}} | collective-permute-start | bytes 4325384 | tf_op jit(solution)/shard_map/ppermute | solution.py:226
  1026.7 362.9 %collective-permute-start.23 = (bf16[2048,2048]{1,0:T(8,128)(2,1)}, bf16[2048,2048]{1,0:T(8,128)(2,1)}, u32[]{:S(2)}, u32[]{:S(2)}) collective-permute-start(bf16[2048,2048]{1,0:T(8,128)(2,1)} %outer_rows.14.after_ref), channel_id=1, source_target_pairs={{0,4},{4,0},{1,5},{5,1},{2,6},{6,2},{3,7},{7,3}} | collective-permute-start | bytes 25165832 | tf_op jit(solution)/shard_map/ppermute | solution.py:296
  1085.7 61.3 %collective-permute-start.22 = (bf16[1408,512]{1,0:T(8,128)(2,1)}, bf16[1408,512]{1,0:T(8,128)(2,1)S(1)}, u32[]{:S(2)}, u32[]{:S(2)}) collective-permute-start(bf16[1408,512]{1,0:T(8,128)(2,1)} %collective-permute-done.21.refs_4_.refs_7_), channel_id=1, source_target_pairs={{0,1},{1,0},{2,3},{3,2},{4,5},{5,4},{6,7},{7,6}} | collective-permute-start | bytes 4325384 | tf_op jit(solution)/shard_map/ppermute | solution.py:226
  1106.4 405.2 %collective-permute-start.29 = (bf16[2048,1408]{1,0:T(8,128)(2,1)}, bf16[2048,1408]{1,0:T(8,128)(2,1)}, u32[]{:S(2)}, u32[]{:S(2)}) collective-permute-start(bf16[2048,1408]{1,0:T(8,128)(2,1)} %collective-permute-done.28.refs_0_), channel_id=1, source_target_pairs={{0,1},{1,0},{2,3},{3,2},{4,5},{5,4},{6,7},{7,6}} | collective-permute-start | bytes 17301512 | tf_op jit(solution)/shard_map/ppermute | solution.py:226
  1146.9 212.6 %collective-permute-start.26 = (bf16[2048,512]{1,0:T(8,128)(2,1)}, bf16[2048,512]{1,0:T(8,128)(2,1)}, u32[]{:S(2)}, u32[]{:S(2)}) collective-permute-start(bf16[2048,512]{1,0:T(8,128)(2,1)} %outer_rows.18.after_ref), channel_id=1, source_target_pairs={{0,4},{4,0},{1,5},{5,1},{2,6},{6,2},{3,7},{7,3}} | collective-permute-start | bytes 6291464 | tf_op jit(solution)/shard_map/ppermute | solution.py:296
  1168.3 131.9 %collective-permute-start.27 = (bf16[2048,512]{1,0:T(8,128)(2,1)}, bf16[2048,512]{1,0:T(8,128)(2,1)}, u32[]{:S(2)}, u32[]{:S(2)}) collective-permute-start(bf16[2048,512]{1,0:T(8,128)(2,1)} %outer_rows.19.after_ref), channel_id=1, source_target_pairs={{0,4},{4,0},{1,5},{5,1},{2,6},{6,2},{3,7},{7,3}} | collective-permute-start | bytes 6291464 | tf_op jit(solution)/shard_map/ppermute | solution.py:296
  1227.7 132.9 %collective-permute-start.25 = (bf16[2048,512]{1,0:T(8,128)(2,1)}, bf16[2048,512]{1,0:T(8,128)(2,1)}, u32[]{:S(2)}, u32[]{:S(2)}) collective-permute-start(bf16[2048,512]{1,0:T(8,128)(2,1)} %outer_rows.17.after_ref), channel_id=1, source_target_pairs={{0,4},{4,0},{1,5},{5,1},{2,6},{6,2},{3,7},{7,3}} | collective-permute-start | bytes 6291464 | tf_op jit(solution)/shard_map/ppermute | solution.py:296
  1300.2 89.4 %collective-permute-start.24 = (bf16[2048,512]{1,0:T(8,128)(2,1)S(1)}, bf16[2048,512]{1,0:T(8,128)(2,1)}, u32[]{:S(2)}, u32[]{:S(2)}) collective-permute-start(bf16[2048,512]{1,0:T(8,128)(2,1)S(1)} %copy-done), channel_id=1, source_target_pairs={{0,4},{4,0},{1,5},{5,1},{2,6},{6,2},{3,7},{7,3}} | collective-permute-start | bytes 6291464 | tf_op jit(solution)/shard_map/ppermute | solution.py:296
  1359.5 261.2 %collective-permute-start.33 = (bf16[1408,2048]{1,0:T(8,128)(2,1)}, bf16[1408,2048]{1,0:T(8,128)(2,1)}, u32[]{:S(2)}, u32[]{:S(2)}) collective-permute-start(bf16[1408,2048]{1,0:T(8,128)(2,1)} %get-tuple-element.28), channel_id=1, source_target_pairs={{0,2},{1,3},{2,0},{3,1},{4,6},{5,7},{6,4},{7,5}} | collective-permute-start | bytes 17301512 | tf_op jit(solution)/shard_map/ppermute | solution.py:223
  1360.6 260.2 %collective-permute-start.35 = (bf16[2048,1408]{1,0:T(8,128)(2,1)}, bf16[2048,1408]{1,0:T(8,128)(2,1)}, u32[]{:S(2)}, u32[]{:S(2)}) collective-permute-start(bf16[2048,1408]{1,0:T(8,128)(2,1)} %get-tuple-element.35), channel_id=1, source_target_pairs={{0,2},{1,3},{2,0},{3,1},{4,6},{5,7},{6,4},{7,5}} | collective-permute-start | bytes 17301512 | tf_op jit(solution)/shard_map/ppermute | solution.py:223
  1389.6 172.0 %collective-permute-start.31 = (bf16[2048,1408]{1,0:T(8,128)(2,1)}, bf16[2048,1408]{1,0:T(8,128)(2,1)}, u32[]{:S(2)}, u32[]{:S(2)}) collective-permute-start(bf16[2048,1408]{1,0:T(8,128)(2,1)} %collective-permute-done.30.refs_2_), channel_id=1, source_target_pairs={{0,1},{1,0},{2,3},{3,2},{4,5},{5,4},{6,7},{7,6}} | collective-permute-start | bytes 17301512 | tf_op jit(solution)/shard_map/ppermute | solution.py:226
  1446.6 287.6 %collective-permute-start.32 = (bf16[2048,2048]{1,0:T(8,128)(2,1)}, bf16[2048,2048]{1,0:T(8,128)(2,1)}, u32[]{:S(2)}, u32[]{:S(2)}) collective-permute-start(bf16[2048,2048]{1,0:T(8,128)(2,1)} %fusion.5.after_ref.rows_ref), channel_id=1, source_target_pairs={{0,4},{4,0},{1,5},{5,1},{2,6},{6,2},{3,7},{7,3}} | collective-permute-start | bytes 25165832 | tf_op jit(solution)/shard_map/ppermute | solution.py:266
  1511.6 222.6 %collective-permute-start.37 = (bf16[2048,1408]{1,0:T(8,128)(2,1)}, bf16[2048,1408]{1,0:T(8,128)(2,1)}, u32[]{:S(2)}, u32[]{:S(2)}) collective-permute-start(bf16[2048,1408]{1,0:T(8,128)(2,1)} %get-tuple-element.31), channel_id=1, source_target_pairs={{0,2},{1,3},{2,0},{3,1},{4,6},{5,7},{6,4},{7,5}} | collective-permute-start | bytes 17301512 | tf_op jit(solution)/shard_map/ppermute | solution.py:223
  1561.7 349.4 %collective-permute-start.39 = (bf16[1408,512]{1,0:T(8,128)(2,1)}, bf16[1408,512]{1,0:T(8,128)(2,1)S(1)}, u32[]{:S(2)}, u32[]{:S(2)}) collective-permute-start(bf16[1408,512]{1,0:T(8,128)(2,1)} %get-tuple-element.42), channel_id=1, source_target_pairs={{0,2},{1,3},{2,0},{3,1},{4,6},{5,7},{6,4},{7,5}} | collective-permute-start | bytes 4325384 | tf_op jit(solution)/shard_map/ppermute | solution.py:223
  1620.7 378.7 %collective-permute-start.41 = (bf16[1408,512]{1,0:T(8,128)(2,1)}, bf16[1408,512]{1,0:T(8,128)(2,1)S(1)}, u32[]{:S(2)}, u32[]{:S(2)}) collective-permute-start(bf16[1408,512]{1,0:T(8,128)(2,1)} %get-tuple-element.41), channel_id=1, source_target_pairs={{0,2},{1,3},{2,0},{3,1},{4,6},{5,7},{6,4},{7,5}} | collective-permute-start | bytes 4325384 | tf_op jit(solution)/shard_map/ppermute | solution.py:223
  1620.8 183.1 %collective-permute-start.34 = (bf16[1408,2048]{1,0:T(8,128)(2,1)}, bf16[1408,2048]{1,0:T(8,128)(2,1)}, u32[]{:S(2)}, u32[]{:S(2)}) collective-permute-start(bf16[1408,2048]{1,0:T(8,128)(2,1)} %collective-permute-done.33.refs_4_), channel_id=1, source_target_pairs={{0,1},{1,0},{2,3},{3,2},{4,5},{5,4},{6,7},{7,6}} | collective-permute-start | bytes 17301512 | tf_op jit(solution)/shard_map/ppermute | solution.py:226
  1734.2 283.9 %collective-permute-start.36 = (bf16[2048,1408]{1,0:T(8,128)(2,1)}, bf16[2048,1408]{1,0:T(8,128)(2,1)}, u32[]{:S(2)}, u32[]{:S(2)}) collective-permute-start(bf16[2048,1408]{1,0:T(8,128)(2,1)} %collective-permute-done.35.refs_0_), channel_id=1, source_target_pairs={{0,1},{1,0},{2,3},{3,2},{4,5},{5,4},{6,7},{7,6}} | collective-permute-start | bytes 17301512 | tf_op jit(solution)/shard_map/ppermute | solution.py:226
  1734.2 283.9 %collective-permute-start.38 = (bf16[2048,1408]{1,0:T(8,128)(2,1)}, bf16[2048,1408]{1,0:T(8,128)(2,1)}, u32[]{:S(2)}, u32[]{:S(2)}) collective-permute-start(bf16[2048,1408]{1,0:T(8,128)(2,1)} %collective-permute-done.37.refs_2_), channel_id=1, source_target_pairs={{0,1},{1,0},{2,3},{3,2},{4,5},{5,4},{6,7},{7,6}} | collective-permute-start | bytes 17301512 | tf_op jit(solution)/shard_map/ppermute | solution.py:226
  1803.9 213.6 %collective-permute-start.43 = (bf16[1408,512]{1,0:T(8,128)(2,1)}, bf16[1408,512]{1,0:T(8,128)(2,1)}, u32[]{:S(2)}, u32[]{:S(2)}) collective-permute-start(bf16[1408,512]{1,0:T(8,128)(2,1)} %get-tuple-element.40), channel_id=1, source_target_pairs={{0,2},{1,3},{2,0},{3,1},{4,6},{5,7},{6,4},{7,5}} | collective-permute-start | bytes 4325384 | tf_op jit(solution)/shard_map/ppermute | solution.py:223
  1911.1 106.5 %collective-permute-start.45 = (bf16[1408,512]{1,0:T(8,128)(2,1)}, bf16[1408,512]{1,0:T(8,128)(2,1)}, u32[]{:S(2)}, u32[]{:S(2)}) collective-permute-start(bf16[1408,512]{1,0:T(8,128)(2,1)} %get-tuple-element.39), channel_id=1, source_target_pairs={{0,2},{1,3},{2,0},{3,1},{4,6},{5,7},{6,4},{7,5}} | collective-permute-start | bytes 4325384 | tf_op jit(solution)/shard_map/ppermute | solution.py:223
  1999.5 33.6 %collective-permute-start.40 = (bf16[1408,512]{1,0:T(8,128)(2,1)S(1)}, bf16[1408,512]{1,0:T(8,128)(2,1)}, u32[]{:S(2)}, u32[]{:S(2)}) collective-permute-start(bf16[1408,512]{1,0:T(8,128)(2,1)S(1)} %collective-permute-done.39.refs_4_), channel_id=1, source_target_pairs={{0,1},{1,0},{2,3},{3,2},{4,5},{5,4},{6,7},{7,6}} | collective-permute-start | bytes 4325384 | tf_op jit(solution)/shard_map/ppermute | solution.py:226
  2017.6 33.6 %collective-permute-start.44 = (bf16[1408,512]{1,0:T(8,128)(2,1)}, bf16[1408,512]{1,0:T(8,128)(2,1)}, u32[]{:S(2)}, u32[]{:S(2)}) collective-permute-start(bf16[1408,512]{1,0:T(8,128)(2,1)} %collective-permute-done.43.refs_4_.refs_6_), channel_id=1, source_target_pairs={{0,1},{1,0},{2,3},{3,2},{4,5},{5,4},{6,7},{7,6}} | collective-permute-start | bytes 4325384 | tf_op jit(solution)/shard_map/ppermute | solution.py:226
  2018.0 43.2 %collective-permute-start.46 = (bf16[1408,512]{1,0:T(8,128)(2,1)}, bf16[1408,512]{1,0:T(8,128)(2,1)}, u32[]{:S(2)}, u32[]{:S(2)}) collective-permute-start(bf16[1408,512]{1,0:T(8,128)(2,1)} %collective-permute-done.45.refs_4_.refs_7_), channel_id=1, source_target_pairs={{0,1},{1,0},{2,3},{3,2},{4,5},{5,4},{6,7},{7,6}} | collective-permute-start | bytes 4325384 | tf_op jit(solution)/shard_map/ppermute | solution.py:226
  2018.1 362.9 %collective-permute-start.47 = (bf16[2048,2048]{1,0:T(8,128)(2,1)}, bf16[2048,2048]{1,0:T(8,128)(2,1)}, u32[]{:S(2)}, u32[]{:S(2)}) collective-permute-start(bf16[2048,2048]{1,0:T(8,128)(2,1)} %outer_rows.21.after_ref), channel_id=1, source_target_pairs={{0,4},{4,0},{1,5},{5,1},{2,6},{6,2},{3,7},{7,3}} | collective-permute-start | bytes 25165832 | tf_op jit(solution)/shard_map/ppermute | solution.py:296
  2041.1 339.9 %collective-permute-start.48 = (bf16[2048,512]{1,0:T(8,128)(2,1)}, bf16[2048,512]{1,0:T(8,128)(2,1)}, u32[]{:S(2)}, u32[]{:S(2)}) collective-permute-start(bf16[2048,512]{1,0:T(8,128)(2,1)} %outer_rows.23.after_ref), channel_id=1, source_target_pairs={{0,4},{4,0},{1,5},{5,1},{2,6},{6,2},{3,7},{7,3}} | collective-permute-start | bytes 6291464 | tf_op jit(solution)/shard_map/ppermute | solution.py:296
  2051.1 329.9 %collective-permute-start.49 = (bf16[2048,512]{1,0:T(8,128)(2,1)}, bf16[2048,512]{1,0:T(8,128)(2,1)S(1)}, u32[]{:S(2)}, u32[]{:S(2)}) collective-permute-start(bf16[2048,512]{1,0:T(8,128)(2,1)} %outer_rows.24.after_ref), channel_id=1, source_target_pairs={{0,4},{4,0},{1,5},{5,1},{2,6},{6,2},{3,7},{7,3}} | collective-permute-start | bytes 6291464 | tf_op jit(solution)/shard_map/ppermute | solution.py:296
  2059.2 321.8 %collective-permute-start.50 = (bf16[2048,512]{1,0:T(8,128)(2,1)}, bf16[2048,512]{1,0:T(8,128)(2,1)}, u32[]{:S(2)}, u32[]{:S(2)}) collective-permute-start(bf16[2048,512]{1,0:T(8,128)(2,1)} %outer_rows.25.after_ref), channel_id=1, source_target_pairs={{0,4},{4,0},{1,5},{5,1},{2,6},{6,2},{3,7},{7,3}} | collective-permute-start | bytes 6291464 | tf_op jit(solution)/shard_map/ppermute | solution.py:296
  2069.2 311.8 %collective-permute-start.51 = (bf16[2048,512]{1,0:T(8,128)(2,1)}, bf16[2048,512]{1,0:T(8,128)(2,1)}, u32[]{:S(2)}, u32[]{:S(2)}) collective-permute-start(bf16[2048,512]{1,0:T(8,128)(2,1)} %outer_rows.26.after_ref), channel_id=1, source_target_pairs={{0,4},{4,0},{1,5},{5,1},{2,6},{6,2},{3,7},{7,3}} | collective-permute-start | bytes 6291464 | tf_op jit(solution)/shard_map/ppermute | solution.py:296
  (21 other events, 1055.1 us)

commit v2 on v1

v2 whole, which is shorter than its diff:
```python
import jax
import jax.numpy as jnp
from jax import lax
from jax.experimental import pallas as pl
from jax.experimental.pallas import tpu as pltpu
from jax.sharding import PartitionSpec as P


NORM_EPS = 1e-5
ROW_TILE = 256
COL_CHUNK = 256
OUT_TILE = 1024
MIX_TILE = 256


def rms_norm(stream, norm_row):
    widened = stream.astype(jnp.float32)
    inv_rms = lax.rsqrt(jnp.mean(widened * widened, axis=-1, keepdims=True) + NORM_EPS)
    return (widened * inv_rms * norm_row).astype(jnp.bfloat16)


def block_order(routes_l, experts):
    tok_dev = routes_l.shape[0]
    ids = jnp.arange(experts, dtype=jnp.int32)
    chosen = (routes_l[:, 0:1] == ids) | (routes_l[:, 1:2] == ids)
    counts = jnp.sum(chosen.astype(jnp.int32), axis=0)
    common = jnp.sum(jnp.where(counts == tok_dev, ids, 0))
    second = routes_l[:, 0] + routes_l[:, 1] - common
    key = second * tok_dev + jnp.arange(tok_dev, dtype=jnp.int32)
    place = jnp.sum((key[:, None] < key[None, :]).astype(jnp.int32), axis=0)
    start = jnp.sum((second[:, None] < ids).astype(jnp.int32), axis=0)
    stop = jnp.sum((second[:, None] <= ids).astype(jnp.int32), axis=0)
    start = jnp.where(ids == common, 0, start)
    stop = jnp.where(ids == common, tok_dev, stop)
    return place, start, stop


def at_place(place, values):
    slots = jnp.arange(place.shape[0], dtype=jnp.int32)
    return jnp.sum(jnp.where(place[:, None] == slots[None, :], values[:, None], 0), axis=0)


def tile_of(step, span):
    return jnp.minimum(span[0] + step, span[1])


def inner_rows(after, span, rows, gates, ups):
    tok, d_model = rows.shape
    part = gates[0][0].shape[-1]
    n_parts = len(gates)
    width = n_parts * part
    sources = list(gates) + list(ups)
    chunks = []
    for first in range(0, width, COL_CHUNK):
        cuts = sorted({first, first + COL_CHUNK} | {q * part for q in range(n_parts) if first < q * part < first + COL_CHUNK})
        chunks.append([(lo // part, lo % part, hi - lo) for lo, hi in zip(cuts, cuts[1:])])

    def kernel(span, after_ref, rows_ref, *refs):
        weight_refs, (act_ref, held, sems) = refs[:len(sources)], refs[len(sources):]
        i = pl.program_id(0)

        def copies(chunk):
            found = []
            for m in range(2):
                for q, first, size in chunks[chunk]:
                    ref, lead = weight_refs[m * n_parts + q], sources[m * n_parts + q][1]
                    at = q * part + first
                    found.append(pltpu.make_async_copy(ref.at[lead + (slice(None), pl.ds(first, size))],
                                                       held.at[m, :, pl.ds(at, size)], sems.at[chunk, len(found)]))
            return found

        @pl.when(i == 0)
        def _():
            for chunk in range(len(chunks)):
                for copy in copies(chunk):
                    copy.start()

        def columns(chunk):
            cols = slice(chunk * COL_CHUNK, (chunk + 1) * COL_CHUNK)
            pre_gate = jnp.dot(rows_ref[...], held[0, :, cols], preferred_element_type=jnp.float32)
            pre_up = jnp.dot(rows_ref[...], held[1, :, cols], preferred_element_type=jnp.float32)
            act_ref[:, cols] = (jax.nn.silu(pre_gate) * pre_up).astype(jnp.bfloat16)

        @pl.when(i == 0)
        def _():
            for chunk in range(len(chunks)):
                for copy in copies(chunk):
                    copy.wait()
                columns(chunk)

        @pl.when((i > 0) & (span[0] + i <= span[1]))
        def _():
            for chunk in range(len(chunks)):
                columns(chunk)

    return pl.pallas_call(
        kernel,
        out_shape=jax.ShapeDtypeStruct((tok, width), jnp.bfloat16),
        grid_spec=pltpu.PrefetchScalarGridSpec(
            num_scalar_prefetch=1, grid=(tok // ROW_TILE,),
            in_specs=[pl.BlockSpec(memory_space=pl.ANY), pl.BlockSpec((ROW_TILE, d_model), lambda i, s: (tile_of(i, s), 0))]
            + [pl.BlockSpec(memory_space=pl.ANY)] * len(sources),
            out_specs=pl.BlockSpec((ROW_TILE, width), lambda i, s: (tile_of(i, s), 0)),
            scratch_shapes=[pltpu.VMEM((2, d_model, width), jnp.bfloat16), pltpu.SemaphoreType.DMA((len(chunks), 2 * n_parts))]),
        compiler_params=pltpu.CompilerParams(dimension_semantics=("arbitrary",)),
        cost_estimate=pl.CostEstimate(flops=2 * tok * d_model * width, bytes_accessed=4 * d_model * width, transcendentals=0),
        name="inner_rows",
    )(span, after, rows, *[s[0] for s in sources])


def outer_rows(after, span, acts, downs):
    tok = acts[0].shape[0]
    depth_all = sum(a.shape[1] for a in acts)
    cols = sum(piece[3] for piece in downs[0][2])
    tile = min(OUT_TILE, cols)
    flat, moves, held_row = [], [[] for _ in range(cols // tile)], 0
    for first_row, rows, pieces in downs:
        at = 0
        for array, lead, first, count in pieces:
            done = 0
            while done < count:
                size = min(count - done, tile - at % tile)
                moves[at // tile].append((len(flat), lead, first_row, rows, first + done, held_row, at % tile, size))
                at, done = at + size, done + size
            flat.append(array)
        held_row += rows
    most = max(len(m) for m in moves)

    def kernel(span, after_ref, *refs):
        act_refs, down_refs = refs[:len(acts)], refs[len(acts):len(acts) + len(flat)]
        out_ref, held, sems = refs[len(acts) + len(flat):]
        c, i = pl.program_id(0), pl.program_id(1)

        def copies(n):
            return [pltpu.make_async_copy(down_refs[a].at[lead + (pl.ds(first_row, rows), pl.ds(first, size))],
                                          held.at[n, pl.ds(row, rows), pl.ds(col, size)], sems.at[n, j])
                    for j, (a, lead, first_row, rows, first, row, col, size) in enumerate(moves[n])]

        @pl.when((c == 0) & (i == 0))
        def _():
            for n in range(len(moves)):
                for copy in copies(n):
                    copy.start()

        for n in range(len(moves)):
            @pl.when((c == n) & (i == 0))
            def _():
                for copy in copies(n):
                    copy.wait()

        @pl.when(span[0] + i <= span[1])
        def _():
            total, at = None, 0
            for act in act_refs:
                depth = act.shape[1]
                term = jnp.dot(act[...], held[c, at:at + depth], preferred_element_type=jnp.float32)
                total = term if total is None else total + term
                at += depth
            out_ref[...] = total.astype(jnp.bfloat16)

    return pl.pallas_call(
        kernel,
        out_shape=jax.ShapeDtypeStruct((tok, cols), jnp.bfloat16),
        grid_spec=pltpu.PrefetchScalarGridSpec(
            num_scalar_prefetch=1, grid=(cols // tile, tok // ROW_TILE),
            in_specs=[pl.BlockSpec(memory_space=pl.ANY)]
            + [pl.BlockSpec((ROW_TILE, a.shape[1]), lambda c, i, s: (tile_of(i, s), 0)) for a in acts]
            + [pl.BlockSpec(memory_space=pl.ANY)] * len(flat),
            out_specs=pl.BlockSpec((ROW_TILE, tile), lambda c, i, s: (tile_of(i, s), c)),
            scratch_shapes=[pltpu.VMEM((len(moves), depth_all, tile), jnp.bfloat16),
                            pltpu.SemaphoreType.DMA((len(moves), most))]),
        compiler_params=pltpu.CompilerParams(dimension_semantics=("arbitrary", "arbitrary")),
        cost_estimate=pl.CostEstimate(flops=tok * cols * depth_all, bytes_accessed=2 * depth_all * cols,
                                      transcendentals=0),
        name="outer_rows",
    )(span, after, *acts, *flat)


def mix(ranges, stream, gates, parts, norm_row=None):
    tok, d_model = stream.shape
    count = len(parts)
    flat = [p for pieces in parts for p in pieces]
    extra = [] if norm_row is None else [norm_row.reshape(1, d_model)]

    def kernel(ranges, stream_ref, gates_ref, *refs):
        outs, total = refs[len(flat) + len(extra):-1], refs[-1]
        first = pl.program_id(0) * MIX_TILE
        row = lax.broadcasted_iota(jnp.int32, (MIX_TILE, 1), 0) + first
        total[...] = stream_ref[...].astype(jnp.float32)
        at = 0
        for e, pieces in enumerate(parts):
            here = refs[at:at + len(pieces)]
            at += len(pieces)

            @pl.when((ranges[e] < first + MIX_TILE) & (ranges[count + e] > first))
            def _():
                picked = (row >= ranges[e]) & (row < ranges[count + e])
                for c, ref in enumerate(here):
                    cols = slice(c * ref.shape[1], (c + 1) * ref.shape[1])
                    total[:, cols] += jnp.where(picked, gates_ref[:, e:e + 1] * ref[...].astype(jnp.float32), 0.0)
        rounded = total[...].astype(jnp.bfloat16)
        outs[0][...] = rounded
        if extra:
            widened = rounded.astype(jnp.float32)
            inv_rms = lax.rsqrt(jnp.sum(widened * widened, axis=-1, keepdims=True) / d_model + NORM_EPS)
            outs[1][...] = (widened * inv_rms * refs[len(flat)][...]).astype(jnp.bfloat16)

    def part_spec(e, cols):
        def tile(i, ranges):
            return jnp.clip(i, ranges[e] // MIX_TILE, (ranges[count + e] - 1) // MIX_TILE), 0

        return pl.BlockSpec((MIX_TILE, cols), tile)

    row_spec = lambda cols: pl.BlockSpec((MIX_TILE, cols), lambda i, s: (i, 0))
    return pl.pallas_call(
        kernel,
        out_shape=[jax.ShapeDtypeStruct((tok, d_model), jnp.bfloat16)] * (1 + len(extra)),
        grid_spec=pltpu.PrefetchScalarGridSpec(
            num_scalar_prefetch=1, grid=(tok // MIX_TILE,),
            in_specs=[row_spec(d_model), row_spec(gates.shape[1])] + [part_spec(e, p.shape[1]) for e, pieces in enumerate(parts) for p in pieces]
            + [pl.BlockSpec((1, d_model), lambda i, s: (0, 0))] * len(extra),
            out_specs=[row_spec(d_model)] * (1 + len(extra)),
            scratch_shapes=[pltpu.VMEM((MIX_TILE, d_model), jnp.float32)]),
        compiler_params=pltpu.CompilerParams(dimension_semantics=("arbitrary",)),
        cost_estimate=pl.CostEstimate(flops=20 * tok * d_model, bytes_accessed=12 * tok * d_model, transcendentals=0),
        name="mix",
    )(ranges, stream, gates, *flat, *extra)


CUTS = (1, 4)
FF_CUTS = (((0, 1408),), ((0, 768), (768, 1408)))


def solution(mesh):
    owners, shards = mesh.shape["ep"], mesh.shape["fsdp"]
    token_spec = P(("rep", "ep", "fsdp"), None)
    expert_in_spec = P(None, "ep", None, "fsdp")
    expert_out_spec = P(None, "ep", "fsdp", None)
    route_spec = P(None, ("rep", "ep", "fsdp"), None)
    swap = [(i, owners - 1 - i) for i in range(owners)]

    def device_step(x_in, norm_w, router_w, gate_w, up_w, down_w, routes):
        layers, tok_dev, _ = routes.shape
        experts = router_w.shape[2]
        n_local = gate_w.shape[1]
        d_model = x_in.shape[1]
        mine = lax.axis_index("ep")

        def across(v):
            return lax.ppermute(v, "fsdp", [(i, (i + shards // 2) % shards) for i in range(shards)])

        def beside(v):
            return lax.ppermute(v, "fsdp", [(i, i ^ 1) for i in range(shards)])

        near = []
        for param in (gate_w, up_w, down_w):
            near.append(beside(param))
        far = [[None] * n_local for _ in range(layers)]
        serial = 0
        for layer in range(layers):
            for k in range(n_local):
                width = d_model // CUTS[k]
                first_gate = lax.optimization_barrier(gate_w) if serial == 0 else gate_w
                pieces = [w[layer, k][:, lo:hi] for lo, hi in FF_CUTS[k] for w in (first_gate, up_w)]
                pieces += [down_w[layer, k][:, c * width:(c + 1) * width] for c in range(CUTS[k])]
                out = []
                for piece in pieces:
                    there = across(piece)
                    out.append((there, beside(there)))
                    serial += 1
                inner = 2 * len(FF_CUTS[k])
                far[layer][k] = (out[0:inner:2], out[1:inner:2], out[inner:])

        orders = [block_order(routes[layer], experts) for layer in range(layers)]
        bounds = jnp.stack([jnp.stack(o[1:]) for o in orders])
        peer_bounds = lax.ppermute(bounds, "ep", swap)
        tokens = jnp.arange(tok_dev, dtype=jnp.int32)

        def spans(table, layer):
            start, stop = table[layer, 0], table[layer, 1]
            both = jnp.stack([start // ROW_TILE, (stop - 1) // ROW_TILE], axis=1)
            return [jnp.where(mine == 0, both[k], both[n_local + k]) for k in range(n_local)]

        def own_first(table):
            return jnp.where(mine == 0, table, jnp.roll(table, n_local, axis=-1))

        stream, hidden = x_in, None
        for layer in range(layers):
            place = orders[layer][0]
            if layer == 0:
                index = at_place(place, tokens)
                stream = stream[index]
                hidden = rms_norm(stream, norm_w[layer])
            else:
                index = at_place(place, orders[layer - 1][0])
                hidden = hidden[index]
            peer_hidden = lax.ppermute(hidden, "ep", swap)
            logits = own_first(jnp.dot(hidden, router_w[layer], preferred_element_type=jnp.float32))
            ranges = own_first(bounds[layer])
            row = tokens[:, None]
            picked = (row >= ranges[0]) & (row < ranges[1])
            top = jnp.max(jnp.where(picked, logits, -jnp.inf), axis=-1, keepdims=True)
            weight = jnp.where(picked, jnp.exp(jnp.where(picked, logits - top, 0.0)), 0.0)
            gates = weight / jnp.sum(weight, axis=-1, keepdims=True)

            own_spans, peer_spans = spans(bounds, layer), spans(peer_bounds, layer)

            def close(after, k, span, rows):
                return inner_rows(after, span, rows, [(gate_w, (layer, k)), (near[0], (layer, k))],
                                  [(up_w, (layer, k)), (near[1], (layer, k))])

            def distant(after, k, span, rows, j):
                gates_far, ups_far, _ = far[layer][k]
                return inner_rows(after, span, rows, [(v, ()) for v in gates_far[j]], [(v, ()) for v in ups_far[j]])

            def outer(after, k, span, acts, pieces):
                down_far = far[layer][k][2]
                ff, cols = down_far[0][0].shape
                first, count = pieces[0] * cols, len(pieces) * cols
                downs = [(0, ff, [(down_w, (layer, k), first, count)]), (0, ff, [(near[2], (layer, k), first, count)])]
                downs += [(lo, hi - lo, [(down_far[c][side], (), 0, cols) for c in pieces]) for lo, hi in FF_CUTS[k] for side in range(2)]
                return outer_rows(after, span, acts, downs)

            def step(make, *args):
                made = make(*args)
                return made

            def send_back(made):
                return lax.ppermute(made, "ep", swap)

            own_close = [hidden]
            for k in range(n_local):
                own_close.append(step(close, own_close[-1], k, own_spans[k], hidden))
            own_far_first = step(distant, own_close[-1], 0, own_spans[0], hidden, 0)
            if layer > 0:
                index, _ = lax.optimization_barrier((index, own_far_first))
                stream = stream[index]
            last = own_far_first if layer == 0 else stream
            own_close, columns = own_close[1:], list(range(CUTS[1]))

            peer_close = [step(close, last, 0, peer_spans[0], peer_hidden)]
            peer_close.append(step(close, peer_close[0], 1, peer_spans[1], peer_hidden))
            peer_far = step(distant, peer_close[1], 0, peer_spans[0], peer_hidden, 0)
            peer_out = step(outer, peer_far, 0, peer_spans[0], [peer_close[0], peer_far], [0])
            back_first = [send_back(peer_out)]
            own_out_first = step(outer, peer_out, 0, own_spans[0], [own_close[0], own_far_first], [0])
            peer_far_second = [step(distant, own_out_first, 1, peer_spans[1], peer_hidden, 0)]
            peer_far_second.append(step(distant, peer_far_second[0], 1, peer_spans[1], peer_hidden, 1))
            last, back_second, own_far = peer_far_second[1], [], []
            for c in columns:
                if c == len(columns) // 2:
                    last = step(distant, last, 1, own_spans[1], hidden, 0)
                    own_far.append(last)
                last = step(outer, last, 1, peer_spans[1], [peer_close[1]] + peer_far_second, [c])
                back_second.append(send_back(last))
            own_far.append(step(distant, last, 1, own_spans[1], hidden, 1))
            own_out_second = step(outer, own_far[1], 1, own_spans[1], [own_close[1]] + own_far, columns)
            parts = [[own_out_first], [own_out_second], back_first, back_second]
            mixed = mix(ranges.reshape(-1), stream, gates, parts, norm_w[layer + 1] if layer + 1 < layers else None)
            stream, hidden = mixed if layer + 1 < layers else (mixed[0], None)
        return stream[orders[layers - 1][0]]

    return jax.shard_map(device_step, mesh=mesh,
                         in_specs=(token_spec, P(), P(), expert_in_spec, expert_in_spec, expert_out_spec, route_spec),
                         out_specs=token_spec, check_vma=False)
```

time: 2430 us -> 2280 us (0.938)
  waiting for transfers between devices: 868 us -> 767 us
  starting transfers between devices: 391 us -> 322 us
  local copies, waits for them, and re-layouts: 127 us -> 166 us
    ppermute x10, waiting for transfers between devices: 317 us -> 226 us  [send_back(): return lax.ppermute(made, 'ep', swap)]
    ppermute x21 -> x25, starting transfers between devices: 214 us -> 129 us  [beside(): return lax.ppermute(v, 'fsdp', [(i, i ^ 1) for i in range(shards)])]
    ppermute x18 -> x22, starting transfers between devices: 169 us -> 184 us  [across(): lax.ppermute(v, 'fsdp', [(i, (i + shards // 2) % shards) for i in range(s...]
    ppermute x18 -> x22, waiting for transfers between devices: 550 us -> 541 us  [across(): lax.ppermute(v, 'fsdp', [(i, (i + shards // 2) % shards) for i in range(s...]
    pallas_call x16 -> x20, Pallas kernels: 590 us -> 581 us  [inner_rows(): pl.pallas_call(kernel, out_shape=jax.ShapeDtypeStruct((tok, width), jnp.b...]
  transfers between devices with their start and end apart: 52 -> 60, of which waited for: 12 -> 10; matrix products, arithmetic and copies ran while one was open for 7% -> 9% of each run, Pallas kernels for 39% -> 41%
where the time goes in v2:
time: 2280 us; the launch traced here: 2270 us
  Pallas kernels  960 us (42%)
  waiting for transfers between devices  767 us (34%)
  starting transfers between devices  322 us (14%)
  local copies, waits for them, and re-layouts  166 us (7%)
  other arithmetic  42.3 us (2%)
    pallas_call x20, Pallas kernels, inner_rows(): pl.pallas_call(kernel, out_shape=jax.ShapeDtypeStruct((tok, width), jnp.b...  581 us
    ppermute x22, waiting for transfers between devices, across(): lax.ppermute(v, 'fsdp', [(i, (i + shards // 2) % shards) for i in range(s...  541 us
    pallas_call x14, Pallas kernels, outer_rows(): pl.pallas_call(kernel, out_shape=jax.ShapeDtypeStruct((tok, cols), jnp.bf...  340 us
    ppermute x10, waiting for transfers between devices, send_back(): return lax.ppermute(made, 'ep', swap)  226 us
    ppermute x22, starting transfers between devices, across(): lax.ppermute(v, 'fsdp', [(i, (i + shards // 2) % shards) for i in range(s...  184 us
    ppermute x25, starting transfers between devices, beside(): return lax.ppermute(v, 'fsdp', [(i, i ^ 1) for i in range(shards)])  129 us
  transfers between devices with their start and end apart: 60, of which 10 were waited for; matrix products, arithmetic and copies ran while one was open for 9% of the time, Pallas kernels for 41%

profile of v2, /device:TPU:0, one launch (start us, length us, event | category | flops | bytes accessed | tf_op | source)
XLA Modules:
  0.0 2271.2 jit_solution(13582373723515476557)
XLA Ops:
  0.9 16.9 slice_bitcast_fusion.2
  39.3 21.2 gather_fusion
  103.1 15.9 slice_bitcast_fusion.1
  119.0 27.2 %collective-permute-done.5.refs_2_ = bf16[2048,1408]{1,0:T(8,128)(2,1)} collective-permute-done((bf16[2048,1408]{1,0:T(8,128)(2,1)}, bf16[2048,1408]{1,0:T(8,128)(2,1)}, u32[]{:S(2)}, u32[]{:S(2)}) %collective-permute-start.5) | collective-permute-done | bytes 5767200 | tf_op jit(solution)/shard_map/ppermute | solution.py:250
  156.7 112.4 %collective-permute-done.3.refs_0_ = bf16[2048,1408]{1,0:T(8,128)(2,1)} collective-permute-done((bf16[2048,1408]{1,0:T(8,128)(2,1)}, bf16[2048,1408]{1,0:T(8,128)(2,1)}, u32[]{:S(2)}, u32[]{:S(2)}) %collective-permute-start.3) | collective-permute-done | bytes 5767200 | tf_op jit(solution)/shard_map/ppermute | solution.py:250
  288.9 56.4 %inner_rows.21.after_ref.refs_0_ = bf16[2048,2816]{1,0:T(8,128)(2,1)} custom-call(s32[2]{0:T(128)} %get-tuple-element.21.span, bf16[2048,2816]{1,0:T(8,128)(2,1)} %inner_rows.20.after_ref.refs_0_, bf16[2048,2048]{1,0:T(8,128)(2,1)} %fusion.2.after_ref.rows_ref, bf16[2,2,2048,1408]{3,2,1,0:T(8,128)(2,1)} %refs_0_.15, ...), custom_call_target="tpu_custom_call" | custom-call | flops 23622320128 | bytes 23068672 | tf_op jit(solution)/shard_map/inner_rows/pallas_call | solution.py:96
  345.3 30.9 %collective-permute-start.13 = (bf16[2048,768]{1,0:T(8,128)(2,1)}, bf16[2048,768]{1,0:T(8,128)(2,1)}, u32[]{:S(2)}, u32[]{:S(2)}) collective-permute-start(bf16[2048,768]{1,0:T(8,128)(2,1)} %slice.332), channel_id=1, source_target_pairs={{0,2},{1,3},{2,0},{3,1},{4,6},{5,7},{6,4},{7,5}} | collective-permute-start | bytes 9437192 | tf_op jit(solution)/shard_map/ppermute | solution.py:250
  401.2 21.4 collective-permute-start.19
  447.1 118.7 %collective-permute-done.19.refs_5_.refs_7_.refs_13_ = bf16[1408,512]{1,0:T(8,128)(2,1)S(1)} collective-permute-done((bf16[1408,512]{1,0:T(8,128)(2,1)S(1)}, bf16[1408,512]{1,0:T(8,128)(2,1)S(1)}, u32[]{:S(2)}, u32[]{:S(2)}) %collective-permute-start.19) | collective-permute-done | bytes 1441824 | tf_op jit(solution)/shard_map/ppermute | solution.py:250
  567.6 56.4 %inner_rows.24.after_ref.refs_0_ = bf16[2048,2816]{1,0:T(8,128)(2,1)} custom-call(s32[2]{0:T(128)} %get-tuple-element.23.span, bf16[2048,2816]{1,0:T(8,128)(2,1)} %inner_rows.23.after_ref.refs_0_, bf16[2048,2048]{1,0:T(8,128)(2,1)} %collective-permute-done.7.rows_ref, bf16[2,2,2048,1408]{3,2,1,0:T(8,128)(2,1)} %refs_0_.15, ...), custom_call_target="tpu_custom_call" | custom-call | flops 23622320128 | bytes 23068672 | tf_op jit(solution)/shard_map/inner_rows/pallas_call | solution.py:96
  640.1 40.9 %collective-permute-start.14 = (bf16[2048,768]{1,0:T(8,128)(2,1)}, bf16[2048,768]{1,0:T(8,128)(2,1)}, u32[]{:S(2)}, u32[]{:S(2)}) collective-permute-start(bf16[2048,768]{1,0:T(8,128)(2,1)} %collective-permute-done.13.refs_2_), channel_id=1, source_target_pairs={{0,1},{1,0},{2,3},{3,2},{4,5},{5,4},{6,7},{7,6}} | collective-permute-start | bytes 9437192 | tf_op jit(solution)/shard_map/ppermute | solution.py:253
  681.0 15.3 outer_rows.14.after_ref
  696.3 72.8 %collective-permute-done.23.refs_5_.refs_7_.refs_15_ = bf16[1408,512]{1,0:T(8,128)(2,1)} collective-permute-done((bf16[1408,512]{1,0:T(8,128)(2,1)}, bf16[1408,512]{1,0:T(8,128)(2,1)}, u32[]{:S(2)}, u32[]{:S(2)}) %collective-permute-start.23) | collective-permute-done | bytes 1441824 | tf_op jit(solution)/shard_map/ppermute | solution.py:250
  769.6 15.1 outer_rows.15.after_ref.refs_0_
  784.8 33.6 %collective-permute-start.34 = (bf16[2048,1408]{1,0:T(8,128)(2,1)}, bf16[2048,1408]{1,0:T(8,128)(2,1)}, u32[]{:S(2)}, u32[]{:S(2)}) collective-permute-start(bf16[2048,1408]{1,0:T(8,128)(2,1)} %get-tuple-element.38), channel_id=1, source_target_pairs={{0,2},{1,3},{2,0},{3,1},{4,6},{5,7},{6,4},{7,5}} | collective-permute-start | bytes 17301512 | tf_op jit(solution)/shard_map/ppermute | solution.py:250
  818.4 33.2 %inner_rows.26.after_ref.refs_1_ = bf16[2048,1536]{1,0:T(8,128)(2,1)} custom-call(s32[2]{0:T(128)} %get-tuple-element.23.span, bf16[2048,2048]{1,0:T(8,128)(2,1)} %outer_rows.15.after_ref.refs_0_, bf16[2048,2048]{1,0:T(8,128)(2,1)} %collective-permute-done.7.rows_ref, bf16[2048,768]{1,0:T(8,128)(2,1)} %collective-permute-done.11.refs_0_, ...), custom_call_target="tpu_custom_call" | custom-call | flops 12884901888 | bytes 12582912 | tf_op jit(solution)/shard_map/inner_rows/pallas_call | solution.py:96
  864.0 28.8 %inner_rows.27.after_ref.refs_2_ = bf16[2048,1280]{1,0:T(8,128)(2,1)} custom-call(s32[2]{0:T(128)} %get-tuple-element.23.span, bf16[2048,1536]{1,0:T(8,128)(2,1)} %inner_rows.26.after_ref.refs_1_, bf16[2048,2048]{1,0:T(8,128)(2,1)} %collective-permute-done.7.rows_ref, bf16[2048,640]{1,0:T(8,128)(2,1)} %collective-permute-done.15.refs_0_, ...), custom_call_target="tpu_custom_call" | custom-call | flops 10737418240 | bytes 10485760 | tf_op jit(solution)/shard_map/inner_rows/pallas_call | solution.py:96
  892.8 20.0 outer_rows.16.after_ref
  912.9 174.8 %collective-permute-done.25.refs_5_.refs_7_.refs_8_.refs_16_ = bf16[1408,512]{1,0:T(8,128)(2,1)S(1)} collective-permute-done((bf16[1408,512]{1,0:T(8,128)(2,1)}, bf16[1408,512]{1,0:T(8,128)(2,1)S(1)}, u32[]{:S(2)}, u32[]{:S(2)}) %collective-permute-start.25) | collective-permute-done | bytes 1441824 | tf_op jit(solution)/shard_map/ppermute | solution.py:250
  1098.0 20.0 outer_rows.17.after_ref
  1118.1 33.7 %inner_rows.28.after_ref.refs_1_ = bf16[2048,1536]{1,0:T(8,128)(2,1)} custom-call(s32[2]{0:T(128)} %get-tuple-element.21.span, bf16[2048,512]{1,0:T(8,128)(2,1)} %outer_rows.17.after_ref, bf16[2048,2048]{1,0:T(8,128)(2,1)} %fusion.2.after_ref.rows_ref, bf16[2048,768]{1,0:T(8,128)(2,1)} %collective-permute-done.11.refs_0_, ...), custom_call_target="tpu_custom_call" | custom-call | flops 12884901888 | bytes 12582912 | tf_op jit(solution)/shard_map/inner_rows/pallas_call | solution.py:96
  1151.8 20.0 outer_rows.18.after_ref
  1173.0 20.0 outer_rows.19.after_ref
  1212.8 28.8 %inner_rows.29.after_ref.refs_2_ = bf16[2048,1280]{1,0:T(8,128)(2,1)} custom-call(s32[2]{0:T(128)} %get-tuple-element.21.span, bf16[2048,512]{1,0:T(8,128)(2,1)} %outer_rows.19.after_ref, bf16[2048,2048]{1,0:T(8,128)(2,1)} %fusion.2.after_ref.rows_ref, bf16[2048,640]{1,0:T(8,128)(2,1)} %collective-permute-done.15.refs_0_, ...), custom_call_target="tpu_custom_call" | custom-call | flops 10737418240 | bytes 10485760 | tf_op jit(solution)/shard_map/inner_rows/pallas_call | solution.py:96
  1241.6 21.0 collective-permute-done.31.refs_6_
  1264.6 59.7 %outer_rows.20.refs_1_ = bf16[2048,2048]{1,0:T(8,128)(2,1)} custom-call(s32[2]{0:T(128)} %get-tuple-element.21.span, bf16[2048,1280]{1,0:T(8,128)(2,1)} %inner_rows.29.after_ref.refs_2_, bf16[2048,2816]{1,0:T(8,128)(2,1)} %inner_rows.21.after_ref.refs_0_, bf16[2048,1536]{1,0:T(8,128)(2,1)} %inner_rows.28.after_ref.refs_1_, ...), custom_call_target="tpu_custom_call" | custom-call | flops 23622320128 | bytes 23068672 | tf_op jit(solution)/shard_map/outer_rows/pallas_call | solution.py:161
  1338.0 20.7 mix.2
  1358.7 20.8 gather_fusion.1
  1379.5 56.1 %inner_rows.30.after_ref.refs_0_ = bf16[2048,2816]{1,0:T(8,128)(2,1)} custom-call(s32[2]{0:T(128)} %get-tuple-element.20.span, bf16[2048,2048]{1,0:T(8,128)(2,1)} %gather_fusion.1, bf16[2048,2048]{1,0:T(8,128)(2,1)} %gather_fusion.1, bf16[2,2,2048,1408]{3,2,1,0:T(8,128)(2,1)} %refs_0_.15, bf16[2,2,2048,1408]{3,2,1,0:T(8,128)(2,1)} %collective-permute-done.1.refs_1_, ...), custom_call_target="tpu_custom_call" | custom-call | flops 23622320128 | bytes 23068672 | tf_op jit(solution)/shard_map/inner_rows/pallas_call | solution.py:96
  1435.6 44.1 %inner_rows.31.after_ref.refs_0_ = bf16[2048,2816]{1,0:T(8,128)(2,1)} custom-call(s32[2]{0:T(128)} %get-tuple-element.19.span, bf16[2048,2816]{1,0:T(8,128)(2,1)} %inner_rows.30.after_ref.refs_0_, bf16[2048,2048]{1,0:T(8,128)(2,1)} %gather_fusion.1, bf16[2,2,2048,1408]{3,2,1,0:T(8,128)(2,1)} %refs_0_.15, ...), custom_call_target="tpu_custom_call" | custom-call | flops 23622320128 | bytes 23068672 | tf_op jit(solution)/shard_map/inner_rows/pallas_call | solution.py:96
  1481.8 56.7 %inner_rows.32.refs_1_ = bf16[2048,2816]{1,0:T(8,128)(2,1)} custom-call(s32[2]{0:T(128)} %get-tuple-element.20.span, bf16[2048,2816]{1,0:T(8,128)(2,1)} %inner_rows.31.after_ref.refs_0_, bf16[2048,2048]{1,0:T(8,128)(2,1)} %gather_fusion.1, bf16[2048,1408]{1,0:T(8,128)(2,1)} %collective-permute-done.32.refs_0_, ...), custom_call_target="tpu_custom_call" | custom-call | flops 23622320128 | bytes 23068672 | tf_op jit(solution)/shard_map/inner_rows/pallas_call | solution.py:96
  1546.4 20.8 gather_fusion.2
  1570.0 25.8 %inner_rows.33.after_ref.refs_0_ = bf16[2048,2816]{1,0:T(8,128)(2,1)} custom-call(s32[2]{0:T(128)} %get-tuple-element.18.span, bf16[2048,2048]{1,0:T(8,128)(2,1)} %gather_fusion.2, bf16[2048,2048]{1,0:T(8,128)(2,1)} %collective-permute-done.36.rows_ref, bf16[2,2,2048,1408]{3,2,1,0:T(8,128)(2,1)} %refs_0_.15, ...), custom_call_target="tpu_custom_call" | custom-call | flops 23622320128 | bytes 23068672 | tf_op jit(solution)/shard_map/inner_rows/pallas_call | solution.py:96
  1609.6 44.9 %collective-permute-start.45 = (bf16[2048,640]{1,0:T(8,128)(2,1)}, bf16[2048,640]{1,0:T(8,128)(2,1)}, u32[]{:S(2)}, u32[]{:S(2)}) collective-permute-start(bf16[2048,640]{1,0:T(8,128)(2,1)} %slice.346), channel_id=1, source_target_pairs={{0,2},{1,3},{2,0},{3,1},{4,6},{5,7},{6,4},{7,5}} | collective-permute-start | bytes 7864328 | tf_op jit(solution)/shard_map/ppermute | solution.py:250
  1654.5 25.7 %inner_rows.35.after_ref.refs_1_ = bf16[2048,2816]{1,0:T(8,128)(2,1)} custom-call(s32[2]{0:T(128)} %get-tuple-element.18.span, bf16[2048,2816]{1,0:T(8,128)(2,1)} %inner_rows.34.after_ref.refs_0_, bf16[2048,2048]{1,0:T(8,128)(2,1)} %collective-permute-done.36.rows_ref, bf16[2048,1408]{1,0:T(8,128)(2,1)} %collective-permute-done.32.refs_0_, ...), custom_call_target="tpu_custom_call" | custom-call | flops 23622320128 | bytes 23068672 | tf_op jit(solution)/shard_map/inner_rows/pallas_call | solution.py:96
  1680.3 32.6 %collective-permute-start.51 = (bf16[1408,512]{1,0:T(8,128)(2,1)}, bf16[1408,512]{1,0:T(8,128)(2,1)}, u32[]{:S(2)}, u32[]{:S(2)}) collective-permute-start(bf16[1408,512]{1,0:T(8,128)(2,1)} %get-tuple-element.45), channel_id=1, source_target_pairs={{0,2},{1,3},{2,0},{3,1},{4,6},{5,7},{6,4},{7,5}} | collective-permute-start | bytes 4325384 | tf_op jit(solution)/shard_map/ppermute | solution.py:250
  1712.8 16.3 collective-permute-start.42
  1729.2 29.9 %outer_rows.21.after_ref = bf16[2048,2048]{1,0:T(8,128)(2,1)} custom-call(s32[2]{0:T(128)} %get-tuple-element.18.span, bf16[2048,2816]{1,0:T(8,128)(2,1)} %inner_rows.35.after_ref.refs_1_, bf16[2048,2816]{1,0:T(8,128)(2,1)} %inner_rows.33.after_ref.refs_0_, bf16[2048,2816]{1,0:T(8,128)(2,1)} %inner_rows.35.after_ref.refs_1_, ...), custom_call_target="tpu_custom_call" | custom-call | flops 23622320128 | bytes 23068672 | tf_op jit(solution)/shard_map/outer_rows/pallas_call | solution.py:161
  1759.1 23.9 %collective-permute-done.51.refs_5_.refs_7_.refs_15_ = bf16[1408,512]{1,0:T(8,128)(2,1)} collective-permute-done((bf16[1408,512]{1,0:T(8,128)(2,1)}, bf16[1408,512]{1,0:T(8,128)(2,1)}, u32[]{:S(2)}, u32[]{:S(2)}) %collective-permute-start.51) | collective-permute-done | bytes 1441824 | tf_op jit(solution)/shard_map/ppermute | solution.py:250
  1790.1 18.9 collective-permute-start.46
  1809.0 59.0 %outer_rows.22.after_ref.refs_0_ = bf16[2048,2048]{1,0:T(8,128)(2,1)} custom-call(s32[2]{0:T(128)} %get-tuple-element.20.span, bf16[2048,2048]{1,0:T(8,128)(2,1)} %outer_rows.21.after_ref, bf16[2048,2816]{1,0:T(8,128)(2,1)} %inner_rows.30.after_ref.refs_0_, bf16[2048,2816]{1,0:T(8,128)(2,1)} %inner_rows.32.refs_1_, bf16[2,2,1408,2048]{3,2,1,0:T(8,128)(2,1)} %refs_3_.19, ...), custom_call_target="tpu_custom_call" | custom-call | flops 23622320128 | bytes 23068672 | tf_op jit(solution)/shard_map/outer_rows/pallas_call | solution.py:161
  1878.0 17.1 collective-permute-start.50
  1922.7 26.6 %inner_rows.38.after_ref.refs_1_ = bf16[2048,1536]{1,0:T(8,128)(2,1)} custom-call(s32[2]{0:T(128)} %get-tuple-element.19.span, bf16[2048,512]{1,0:T(8,128)(2,1)} %outer_rows.24.after_ref, bf16[2048,2048]{1,0:T(8,128)(2,1)} %gather_fusion.1, bf16[2048,768]{1,0:T(8,128)(2,1)} %collective-permute-done.39.refs_0_, ...), custom_call_target="tpu_custom_call" | custom-call | flops 12884901888 | bytes 12582912 | tf_op jit(solution)/shard_map/inner_rows/pallas_call | solution.py:96
  1967.6 22.9 %inner_rows.39.after_ref.refs_2_ = bf16[2048,1280]{1,0:T(8,128)(2,1)} custom-call(s32[2]{0:T(128)} %get-tuple-element.19.span, bf16[2048,512]{1,0:T(8,128)(2,1)} %outer_rows.26.after_ref, bf16[2048,2048]{1,0:T(8,128)(2,1)} %gather_fusion.1, bf16[2048,640]{1,0:T(8,128)(2,1)} %collective-permute-done.43.refs_0_, ...), custom_call_target="tpu_custom_call" | custom-call | flops 10737418240 | bytes 10485760 | tf_op jit(solution)/shard_map/inner_rows/pallas_call | solution.py:96
  1990.5 49.0 %outer_rows.27.refs_1_ = bf16[2048,2048]{1,0:T(8,128)(2,1)} custom-call(s32[2]{0:T(128)} %get-tuple-element.19.span, bf16[2048,1280]{1,0:T(8,128)(2,1)} %inner_rows.39.after_ref.refs_2_, bf16[2048,2816]{1,0:T(8,128)(2,1)} %inner_rows.31.after_ref.refs_0_, bf16[2048,1536]{1,0:T(8,128)(2,1)} %inner_rows.38.after_ref.refs_1_, ...), custom_call_target="tpu_custom_call" | custom-call | flops 23622320128 | bytes 23068672 | tf_op jit(solution)/shard_map/outer_rows/pallas_call | solution.py:161
  2039.5 191.6 %collective-permute-done.59.refs_6_ = bf16[2048,512]{1,0:T(8,128)(2,1)} collective-permute-done((bf16[2048,512]{1,0:T(8,128)(2,1)}, bf16[2048,512]{1,0:T(8,128)(2,1)}, u32[]{:S(2)}, u32[]{:S(2)}) %collective-permute-start.59) | collective-permute-done | bytes 2097184 | tf_op jit(solution)/shard_map/ppermute | solution.py:329
  2232.4 17.9 mix.3
  2250.3 20.8 gather_fusion.3
  (256 shorter events, 312.8 us)
Async XLA Ops:
  0.0 269.1 %collective-permute-start.1 = (bf16[2,2,2048,1408]{3,2,1,0:T(8,128)(2,1)}, bf16[2,2,2048,1408]{3,2,1,0:T(8,128)(2,1)}, u32[]{:S(2)}, u32[]{:S(2)}) collective-permute-start(bf16[2,2,2048,1408]{3,2,1,0:T(8,128)(2,1)} %refs_0_.15), channel_id=1, source_target_pairs={{0,1},{1,0},{2,3},{3,2},{4,5},{5,4},{6,7},{7,6}} | collective-permute-start | bytes 69206024 | tf_op jit(solution)/shard_map/ppermute | solution.py:253
  0.8 272.9 %collective-permute-start.2 = (bf16[2,2,2048,1408]{3,2,1,0:T(8,128)(2,1)}, bf16[2,2,2048,1408]{3,2,1,0:T(8,128)(2,1)}, u32[]{:S(2)}, u32[]{:S(2)}) collective-permute-start(bf16[2,2,2048,1408]{3,2,1,0:T(8,128)(2,1)} %refs_2_.21), channel_id=1, source_target_pairs={{0,1},{1,0},{2,3},{3,2},{4,5},{5,4},{6,7},{7,6}} | collective-permute-start | bytes 69206024 | tf_op jit(solution)/shard_map/ppermute | solution.py:253
  17.7 128.4 %collective-permute-start.5 = (bf16[2048,1408]{1,0:T(8,128)(2,1)}, bf16[2048,1408]{1,0:T(8,128)(2,1)}, u32[]{:S(2)}, u32[]{:S(2)}) collective-permute-start(bf16[2048,1408]{1,0:T(8,128)(2,1)} %get-tuple-element.40), channel_id=1, source_target_pairs={{0,2},{1,3},{2,0},{3,1},{4,6},{5,7},{6,4},{7,5}} | collective-permute-start | bytes 17301512 | tf_op jit(solution)/shard_map/ppermute | solution.py:250
  28.4 652.6 %collective-permute-start.8 = (bf16[2,2,1408,2048]{3,2,1,0:T(8,128)(2,1)}, bf16[2,2,1408,2048]{3,2,1,0:T(8,128)(2,1)}, u32[]{:S(2)}, u32[]{:S(2)}) collective-permute-start(bf16[2,2,1408,2048]{3,2,1,0:T(8,128)(2,1)} %refs_3_.19), channel_id=1, source_target_pairs={{0,1},{1,0},{2,3},{3,2},{4,5},{5,4},{6,7},{7,6}} | collective-permute-start | bytes 69206024 | tf_op jit(solution)/shard_map/ppermute | solution.py:253
  88.9 180.2 %collective-permute-start.3 = (bf16[2048,1408]{1,0:T(8,128)(2,1)}, bf16[2048,1408]{1,0:T(8,128)(2,1)}, u32[]{:S(2)}, u32[]{:S(2)}) collective-permute-start(bf16[2048,1408]{1,0:T(8,128)(2,1)} %slice_bitcast_fusion), channel_id=1, source_target_pairs={{0,2},{1,3},{2,0},{3,1},{4,6},{5,7},{6,4},{7,5}} | collective-permute-start | bytes 17301512 | tf_op jit(solution)/shard_map/ppermute | solution.py:250
  146.2 276.5 %collective-permute-start.7 = (bf16[2048,2048]{1,0:T(8,128)(2,1)}, bf16[2048,2048]{1,0:T(8,128)(2,1)}, u32[]{:S(2)}, u32[]{:S(2)}) collective-permute-start(bf16[2048,2048]{1,0:T(8,128)(2,1)} %fusion.2.after_ref.rows_ref), channel_id=1, source_target_pairs={{0,4},{4,0},{1,5},{5,1},{2,6},{6,2},{3,7},{7,3}} | collective-permute-start | bytes 25165832 | tf_op jit(solution)/shard_map/ppermute | solution.py:297
  269.1 107.2 %collective-permute-start.4 = (bf16[2048,1408]{1,0:T(8,128)(2,1)}, bf16[2048,1408]{1,0:T(8,128)(2,1)}, u32[]{:S(2)}, u32[]{:S(2)}) collective-permute-start(bf16[2048,1408]{1,0:T(8,128)(2,1)} %collective-permute-done.3.refs_0_), channel_id=1, source_target_pairs={{0,1},{1,0},{2,3},{3,2},{4,5},{5,4},{6,7},{7,6}} | collective-permute-start | bytes 17301512 | tf_op jit(solution)/shard_map/ppermute | solution.py:253
  273.8 127.5 %collective-permute-start.9 = (bf16[1408,2048]{1,0:T(8,128)(2,1)}, bf16[1408,2048]{1,0:T(8,128)(2,1)}, u32[]{:S(2)}, u32[]{:S(2)}) collective-permute-start(bf16[1408,2048]{1,0:T(8,128)(2,1)} %get-tuple-element.36), channel_id=1, source_target_pairs={{0,2},{1,3},{2,0},{3,1},{4,6},{5,7},{6,4},{7,5}} | collective-permute-start | bytes 17301512 | tf_op jit(solution)/shard_map/ppermute | solution.py:250
  345.3 279.0 %collective-permute-start.13 = (bf16[2048,768]{1,0:T(8,128)(2,1)}, bf16[2048,768]{1,0:T(8,128)(2,1)}, u32[]{:S(2)}, u32[]{:S(2)}) collective-permute-start(bf16[2048,768]{1,0:T(8,128)(2,1)} %slice.332), channel_id=1, source_target_pairs={{0,2},{1,3},{2,0},{3,1},{4,6},{5,7},{6,4},{7,5}} | collective-permute-start | bytes 9437192 | tf_op jit(solution)/shard_map/ppermute | solution.py:250
  376.3 263.5 %collective-permute-start.11 = (bf16[2048,768]{1,0:T(8,128)(2,1)}, bf16[2048,768]{1,0:T(8,128)(2,1)}, u32[]{:S(2)}, u32[]{:S(2)}) collective-permute-start(bf16[2048,768]{1,0:T(8,128)(2,1)} %slice.331), channel_id=1, source_target_pairs={{0,2},{1,3},{2,0},{3,1},{4,6},{5,7},{6,4},{7,5}} | collective-permute-start | bytes 9437192 | tf_op jit(solution)/shard_map/ppermute | solution.py:250
  401.2 164.7 %collective-permute-start.19 = (bf16[1408,512]{1,0:T(8,128)(2,1)S(1)}, bf16[1408,512]{1,0:T(8,128)(2,1)S(1)}, u32[]{:S(2)}, u32[]{:S(2)}) collective-permute-start(bf16[1408,512]{1,0:T(8,128)(2,1)S(1)} %get-tuple-element.51), channel_id=1, source_target_pairs={{0,2},{1,3},{2,0},{3,1},{4,6},{5,7},{6,4},{7,5}} | collective-permute-start | bytes 4325384 | tf_op jit(solution)/shard_map/ppermute | solution.py:250
  422.7 217.4 %collective-permute-start.10 = (bf16[1408,2048]{1,0:T(8,128)(2,1)}, bf16[1408,2048]{1,0:T(8,128)(2,1)}, u32[]{:S(2)}, u32[]{:S(2)}) collective-permute-start(bf16[1408,2048]{1,0:T(8,128)(2,1)} %collective-permute-done.9.refs_4_), channel_id=1, source_target_pairs={{0,1},{1,0},{2,3},{3,2},{4,5},{5,4},{6,7},{7,6}} | collective-permute-start | bytes 17301512 | tf_op jit(solution)/shard_map/ppermute | solution.py:253
  624.0 145.1 %collective-permute-start.17 = (bf16[2048,640]{1,0:T(8,128)(2,1)}, bf16[2048,640]{1,0:T(8,128)(2,1)}, u32[]{:S(2)}, u32[]{:S(2)}) collective-permute-start(bf16[2048,640]{1,0:T(8,128)(2,1)} %slice.334), channel_id=1, source_target_pairs={{0,2},{1,3},{2,0},{3,1},{4,6},{5,7},{6,4},{7,5}} | collective-permute-start | bytes 7864328 | tf_op jit(solution)/shard_map/ppermute | solution.py:250
  624.3 145.3 %collective-permute-start.15 = (bf16[2048,640]{1,0:T(8,128)(2,1)}, bf16[2048,640]{1,0:T(8,128)(2,1)}, u32[]{:S(2)}, u32[]{:S(2)}) collective-permute-start(bf16[2048,640]{1,0:T(8,128)(2,1)} %slice.333), channel_id=1, source_target_pairs={{0,2},{1,3},{2,0},{3,1},{4,6},{5,7},{6,4},{7,5}} | collective-permute-start | bytes 7864328 | tf_op jit(solution)/shard_map/ppermute | solution.py:250
  639.8 129.3 %collective-permute-start.23 = (bf16[1408,512]{1,0:T(8,128)(2,1)}, bf16[1408,512]{1,0:T(8,128)(2,1)}, u32[]{:S(2)}, u32[]{:S(2)}) collective-permute-start(bf16[1408,512]{1,0:T(8,128)(2,1)} %get-tuple-element.49), channel_id=1, source_target_pairs={{0,2},{1,3},{2,0},{3,1},{4,6},{5,7},{6,4},{7,5}} | collective-permute-start | bytes 4325384 | tf_op jit(solution)/shard_map/ppermute | solution.py:250
  640.1 144.7 %collective-permute-start.14 = (bf16[2048,768]{1,0:T(8,128)(2,1)}, bf16[2048,768]{1,0:T(8,128)(2,1)}, u32[]{:S(2)}, u32[]{:S(2)}) collective-permute-start(bf16[2048,768]{1,0:T(8,128)(2,1)} %collective-permute-done.13.refs_2_), channel_id=1, source_target_pairs={{0,1},{1,0},{2,3},{3,2},{4,5},{5,4},{6,7},{7,6}} | collective-permute-start | bytes 9437192 | tf_op jit(solution)/shard_map/ppermute | solution.py:253
  681.0 137.4 %collective-permute-start.12 = (bf16[2048,768]{1,0:T(8,128)(2,1)}, bf16[2048,768]{1,0:T(8,128)(2,1)}, u32[]{:S(2)}, u32[]{:S(2)}) collective-permute-start(bf16[2048,768]{1,0:T(8,128)(2,1)} %collective-permute-done.11.refs_0_), channel_id=1, source_target_pairs={{0,1},{1,0},{2,3},{3,2},{4,5},{5,4},{6,7},{7,6}} | collective-permute-start | bytes 9437192 | tf_op jit(solution)/shard_map/ppermute | solution.py:253
  769.1 82.6 %collective-permute-start.20 = (bf16[1408,512]{1,0:T(8,128)(2,1)S(1)}, bf16[1408,512]{1,0:T(8,128)(2,1)}, u32[]{:S(2)}, u32[]{:S(2)}) collective-permute-start(bf16[1408,512]{1,0:T(8,128)(2,1)S(1)} %collective-permute-done.19.refs_5_.refs_7_.refs_13_), channel_id=1, source_target_pairs={{0,1},{1,0},{2,3},{3,2},{4,5},{5,4},{6,7},{7,6}} | collective-permute-start | bytes 4325384 | tf_op jit(solution)/shard_map/ppermute | solution.py:253
  769.1 84.6 %collective-permute-start.18 = (bf16[2048,640]{1,0:T(8,128)(2,1)}, bf16[2048,640]{1,0:T(8,128)(2,1)}, u32[]{:S(2)}, u32[]{:S(2)}) collective-permute-start(bf16[2048,640]{1,0:T(8,128)(2,1)} %collective-permute-done.17.refs_2_), channel_id=1, source_target_pairs={{0,1},{1,0},{2,3},{3,2},{4,5},{5,4},{6,7},{7,6}} | collective-permute-start | bytes 7864328 | tf_op jit(solution)/shard_map/ppermute | solution.py:253
  769.6 94.4 %collective-permute-start.16 = (bf16[2048,640]{1,0:T(8,128)(2,1)}, bf16[2048,640]{1,0:T(8,128)(2,1)}, u32[]{:S(2)}, u32[]{:S(2)}) collective-permute-start(bf16[2048,640]{1,0:T(8,128)(2,1)} %collective-permute-done.15.refs_0_), channel_id=1, source_target_pairs={{0,1},{1,0},{2,3},{3,2},{4,5},{5,4},{6,7},{7,6}} | collective-permute-start | bytes 7864328 | tf_op jit(solution)/shard_map/ppermute | solution.py:253
  784.8 427.6 %collective-permute-start.34 = (bf16[2048,1408]{1,0:T(8,128)(2,1)}, bf16[2048,1408]{1,0:T(8,128)(2,1)}, u32[]{:S(2)}, u32[]{:S(2)}) collective-permute-start(bf16[2048,1408]{1,0:T(8,128)(2,1)} %get-tuple-element.38), channel_id=1, source_target_pairs={{0,2},{1,3},{2,0},{3,1},{4,6},{5,7},{6,4},{7,5}} | collective-permute-start | bytes 17301512 | tf_op jit(solution)/shard_map/ppermute | solution.py:250
  818.4 394.0 %collective-permute-start.32 = (bf16[2048,1408]{1,0:T(8,128)(2,1)}, bf16[2048,1408]{1,0:T(8,128)(2,1)}, u32[]{:S(2)}, u32[]{:S(2)}) collective-permute-start(bf16[2048,1408]{1,0:T(8,128)(2,1)} %get-tuple-element.42), channel_id=1, source_target_pairs={{0,2},{1,3},{2,0},{3,1},{4,6},{5,7},{6,4},{7,5}} | collective-permute-start | bytes 17301512 | tf_op jit(solution)/shard_map/ppermute | solution.py:250
  851.6 236.0 %collective-permute-start.25 = (bf16[1408,512]{1,0:T(8,128)(2,1)}, bf16[1408,512]{1,0:T(8,128)(2,1)S(1)}, u32[]{:S(2)}, u32[]{:S(2)}) collective-permute-start(bf16[1408,512]{1,0:T(8,128)(2,1)} %get-tuple-element.48), channel_id=1, source_target_pairs={{0,2},{1,3},{2,0},{3,1},{4,6},{5,7},{6,4},{7,5}} | collective-permute-start | bytes 4325384 | tf_op jit(solution)/shard_map/ppermute | solution.py:250
  853.7 244.4 %collective-permute-start.22 = (bf16[1408,512]{1,0:T(8,128)(2,1)S(1)}, bf16[1408,512]{1,0:T(8,128)(2,1)}, u32[]{:S(2)}, u32[]{:S(2)}) collective-permute-start(bf16[1408,512]{1,0:T(8,128)(2,1)S(1)} %collective-permute-done.21.refs_5_.refs_7_.refs_6_.refs_14_), channel_id=1, source_target_pairs={{0,1},{1,0},{2,3},{3,2},{4,5},{5,4},{6,7},{7,6}} | collective-permute-start | bytes 4325384 | tf_op jit(solution)/shard_map/ppermute | solution.py:253
  864.0 474.0 %collective-permute-start.27 = (bf16[2048,2048]{1,0:T(8,128)(2,1)}, bf16[2048,2048]{1,0:T(8,128)(2,1)}, u32[]{:S(2)}, u32[]{:S(2)}) collective-permute-start(bf16[2048,2048]{1,0:T(8,128)(2,1)} %outer_rows.14.after_ref), channel_id=1, source_target_pairs={{0,4},{4,0},{1,5},{5,1},{2,6},{6,2},{3,7},{7,3}} | collective-permute-start | bytes 25165832 | tf_op jit(solution)/shard_map/ppermute | solution.py:329
  1171.9 90.8 %collective-permute-start.30 = (bf16[2048,512]{1,0:T(8,128)(2,1)}, bf16[2048,512]{1,0:T(8,128)(2,1)}, u32[]{:S(2)}, u32[]{:S(2)}) collective-permute-start(bf16[2048,512]{1,0:T(8,128)(2,1)} %outer_rows.18.after_ref), channel_id=1, source_target_pairs={{0,4},{4,0},{1,5},{5,1},{2,6},{6,2},{3,7},{7,3}} | collective-permute-start | bytes 6291464 | tf_op jit(solution)/shard_map/ppermute | solution.py:329
  1212.3 267.4 %collective-permute-start.35 = (bf16[2048,1408]{1,0:T(8,128)(2,1)}, bf16[2048,1408]{1,0:T(8,128)(2,1)}, u32[]{:S(2)}, u32[]{:S(2)}) collective-permute-start(bf16[2048,1408]{1,0:T(8,128)(2,1)} %collective-permute-done.34.refs_2_), channel_id=1, source_target_pairs={{0,1},{1,0},{2,3},{3,2},{4,5},{5,4},{6,7},{7,6}} | collective-permute-start | bytes 17301512 | tf_op jit(solution)/shard_map/ppermute | solution.py:253
  1212.3 267.5 %collective-permute-start.33 = (bf16[2048,1408]{1,0:T(8,128)(2,1)}, bf16[2048,1408]{1,0:T(8,128)(2,1)}, u32[]{:S(2)}, u32[]{:S(2)}) collective-permute-start(bf16[2048,1408]{1,0:T(8,128)(2,1)} %collective-permute-done.32.refs_0_), channel_id=1, source_target_pairs={{0,1},{1,0},{2,3},{3,2},{4,5},{5,4},{6,7},{7,6}} | collective-permute-start | bytes 17301512 | tf_op jit(solution)/shard_map/ppermute | solution.py:253
  1324.4 245.6 %collective-permute-start.37 = (bf16[1408,2048]{1,0:T(8,128)(2,1)}, bf16[1408,2048]{1,0:T(8,128)(2,1)}, u32[]{:S(2)}, u32[]{:S(2)}) collective-permute-start(bf16[1408,2048]{1,0:T(8,128)(2,1)} %get-tuple-element.34), channel_id=1, source_target_pairs={{0,2},{1,3},{2,0},{3,1},{4,6},{5,7},{6,4},{7,5}} | collective-permute-start | bytes 17301512 | tf_op jit(solution)/shard_map/ppermute | solution.py:250
  1338.0 342.3 %collective-permute-start.41 = (bf16[2048,768]{1,0:T(8,128)(2,1)}, bf16[2048,768]{1,0:T(8,128)(2,1)}, u32[]{:S(2)}, u32[]{:S(2)}) collective-permute-start(bf16[2048,768]{1,0:T(8,128)(2,1)} %slice.344), channel_id=1, source_target_pairs={{0,2},{1,3},{2,0},{3,1},{4,6},{5,7},{6,4},{7,5}} | collective-permute-start | bytes 9437192 | tf_op jit(solution)/shard_map/ppermute | solution.py:250
  1379.5 190.5 %collective-permute-start.36 = (bf16[2048,2048]{1,0:T(8,128)(2,1)}, bf16[2048,2048]{1,0:T(8,128)(2,1)}, u32[]{:S(2)}, u32[]{:S(2)}) collective-permute-start(bf16[2048,2048]{1,0:T(8,128)(2,1)} %gather_fusion.1), channel_id=1, source_target_pairs={{0,4},{4,0},{1,5},{5,1},{2,6},{6,2},{3,7},{7,3}} | collective-permute-start | bytes 25165832 | tf_op jit(solution)/shard_map/ppermute | solution.py:297
  1479.8 233.1 %collective-permute-start.39 = (bf16[2048,768]{1,0:T(8,128)(2,1)}, bf16[2048,768]{1,0:T(8,128)(2,1)}, u32[]{:S(2)}, u32[]{:S(2)}) collective-permute-start(bf16[2048,768]{1,0:T(8,128)(2,1)} %slice.343), channel_id=1, source_target_pairs={{0,2},{1,3},{2,0},{3,1},{4,6},{5,7},{6,4},{7,5}} | collective-permute-start | bytes 9437192 | tf_op jit(solution)/shard_map/ppermute | solution.py:250
  1479.8 129.7 %collective-permute-start.47 = (bf16[1408,512]{1,0:T(8,128)(2,1)}, bf16[1408,512]{1,0:T(8,128)(2,1)S(1)}, u32[]{:S(2)}, u32[]{:S(2)}) collective-permute-start(bf16[1408,512]{1,0:T(8,128)(2,1)} %get-tuple-element.47), channel_id=1, source_target_pairs={{0,2},{1,3},{2,0},{3,1},{4,6},{5,7},{6,4},{7,5}} | collective-permute-start | bytes 4325384 | tf_op jit(solution)/shard_map/ppermute | solution.py:250
  1570.0 84.5 %collective-permute-start.49 = (bf16[1408,512]{1,0:T(8,128)(2,1)}, bf16[1408,512]{1,0:T(8,128)(2,1)S(1)}, u32[]{:S(2)}, u32[]{:S(2)}) collective-permute-start(bf16[1408,512]{1,0:T(8,128)(2,1)} %get-tuple-element.46), channel_id=1, source_target_pairs={{0,2},{1,3},{2,0},{3,1},{4,6},{5,7},{6,4},{7,5}} | collective-permute-start | bytes 4325384 | tf_op jit(solution)/shard_map/ppermute | solution.py:250
  1570.0 159.1 %collective-permute-start.38 = (bf16[1408,2048]{1,0:T(8,128)(2,1)}, bf16[1408,2048]{1,0:T(8,128)(2,1)}, u32[]{:S(2)}, u32[]{:S(2)}) collective-permute-start(bf16[1408,2048]{1,0:T(8,128)(2,1)} %collective-permute-done.37.refs_4_), channel_id=1, source_target_pairs={{0,1},{1,0},{2,3},{3,2},{4,5},{5,4},{6,7},{7,6}} | collective-permute-start | bytes 17301512 | tf_op jit(solution)/shard_map/ppermute | solution.py:253
  1609.6 180.5 %collective-permute-start.45 = (bf16[2048,640]{1,0:T(8,128)(2,1)}, bf16[2048,640]{1,0:T(8,128)(2,1)}, u32[]{:S(2)}, u32[]{:S(2)}) collective-permute-start(bf16[2048,640]{1,0:T(8,128)(2,1)} %slice.346), channel_id=1, source_target_pairs={{0,2},{1,3},{2,0},{3,1},{4,6},{5,7},{6,4},{7,5}} | collective-permute-start | bytes 7864328 | tf_op jit(solution)/shard_map/ppermute | solution.py:250
  1654.5 154.5 %collective-permute-start.43 = (bf16[2048,640]{1,0:T(8,128)(2,1)}, bf16[2048,640]{1,0:T(8,128)(2,1)}, u32[]{:S(2)}, u32[]{:S(2)}) collective-permute-start(bf16[2048,640]{1,0:T(8,128)(2,1)} %slice.345), channel_id=1, source_target_pairs={{0,2},{1,3},{2,0},{3,1},{4,6},{5,7},{6,4},{7,5}} | collective-permute-start | bytes 7864328 | tf_op jit(solution)/shard_map/ppermute | solution.py:250
  1680.3 102.7 %collective-permute-start.51 = (bf16[1408,512]{1,0:T(8,128)(2,1)}, bf16[1408,512]{1,0:T(8,128)(2,1)}, u32[]{:S(2)}, u32[]{:S(2)}) collective-permute-start(bf16[1408,512]{1,0:T(8,128)(2,1)} %get-tuple-element.45), channel_id=1, source_target_pairs={{0,2},{1,3},{2,0},{3,1},{4,6},{5,7},{6,4},{7,5}} | collective-permute-start | bytes 4325384 | tf_op jit(solution)/shard_map/ppermute | solution.py:250
  1712.8 155.2 %collective-permute-start.42 = (bf16[2048,768]{1,0:T(8,128)(2,1)}, bf16[2048,768]{1,0:T(8,128)(2,1)}, u32[]{:S(2)}, u32[]{:S(2)}) collective-permute-start(bf16[2048,768]{1,0:T(8,128)(2,1)} %collective-permute-done.41.refs_2_), channel_id=1, source_target_pairs={{0,1},{1,0},{2,3},{3,2},{4,5},{5,4},{6,7},{7,6}} | collective-permute-start | bytes 9437192 | tf_op jit(solution)/shard_map/ppermute | solution.py:253
  1729.1 139.4 %collective-permute-start.40 = (bf16[2048,768]{1,0:T(8,128)(2,1)}, bf16[2048,768]{1,0:T(8,128)(2,1)}, u32[]{:S(2)}, u32[]{:S(2)}) collective-permute-start(bf16[2048,768]{1,0:T(8,128)(2,1)} %collective-permute-done.39.refs_0_), channel_id=1, source_target_pairs={{0,1},{1,0},{2,3},{3,2},{4,5},{5,4},{6,7},{7,6}} | collective-permute-start | bytes 9437192 | tf_op jit(solution)/shard_map/ppermute | solution.py:253
  1783.0 95.0 %collective-permute-start.53 = (bf16[1408,512]{1,0:T(8,128)(2,1)}, bf16[1408,512]{1,0:T(8,128)(2,1)}, u32[]{:S(2)}, u32[]{:S(2)}) collective-permute-start(bf16[1408,512]{1,0:T(8,128)(2,1)} %get-tuple-element.44), channel_id=1, source_target_pairs={{0,2},{1,3},{2,0},{3,1},{4,6},{5,7},{6,4},{7,5}} | collective-permute-start | bytes 4325384 | tf_op jit(solution)/shard_map/ppermute | solution.py:250
  1790.1 105.0 %collective-permute-start.46 = (bf16[2048,640]{1,0:T(8,128)(2,1)}, bf16[2048,640]{1,0:T(8,128)(2,1)}, u32[]{:S(2)}, u32[]{:S(2)}) collective-permute-start(bf16[2048,640]{1,0:T(8,128)(2,1)} %collective-permute-done.45.refs_2_), channel_id=1, source_target_pairs={{0,1},{1,0},{2,3},{3,2},{4,5},{5,4},{6,7},{7,6}} | collective-permute-start | bytes 7864328 | tf_op jit(solution)/shard_map/ppermute | solution.py:253
  1809.0 86.1 %collective-permute-start.44 = (bf16[2048,640]{1,0:T(8,128)(2,1)}, bf16[2048,640]{1,0:T(8,128)(2,1)}, u32[]{:S(2)}, u32[]{:S(2)}) collective-permute-start(bf16[2048,640]{1,0:T(8,128)(2,1)} %collective-permute-done.43.refs_0_), channel_id=1, source_target_pairs={{0,1},{1,0},{2,3},{3,2},{4,5},{5,4},{6,7},{7,6}} | collective-permute-start | bytes 7864328 | tf_op jit(solution)/shard_map/ppermute | solution.py:253
  1868.6 362.5 %collective-permute-start.55 = (bf16[2048,2048]{1,0:T(8,128)(2,1)}, bf16[2048,2048]{1,0:T(8,128)(2,1)}, u32[]{:S(2)}, u32[]{:S(2)}) collective-permute-start(bf16[2048,2048]{1,0:T(8,128)(2,1)} %outer_rows.21.after_ref), channel_id=1, source_target_pairs={{0,4},{4,0},{1,5},{5,1},{2,6},{6,2},{3,7},{7,3}} | collective-permute-start | bytes 25165832 | tf_op jit(solution)/shard_map/ppermute | solution.py:329
  1912.6 318.5 %collective-permute-start.56 = (bf16[2048,512]{1,0:T(8,128)(2,1)}, bf16[2048,512]{1,0:T(8,128)(2,1)}, u32[]{:S(2)}, u32[]{:S(2)}) collective-permute-start(bf16[2048,512]{1,0:T(8,128)(2,1)} %outer_rows.23.after_ref), channel_id=1, source_target_pairs={{0,4},{4,0},{1,5},{5,1},{2,6},{6,2},{3,7},{7,3}} | collective-permute-start | bytes 6291464 | tf_op jit(solution)/shard_map/ppermute | solution.py:329
  1920.7 310.4 %collective-permute-start.57 = (bf16[2048,512]{1,0:T(8,128)(2,1)}, bf16[2048,512]{1,0:T(8,128)(2,1)S(1)}, u32[]{:S(2)}, u32[]{:S(2)}) collective-permute-start(bf16[2048,512]{1,0:T(8,128)(2,1)} %outer_rows.24.after_ref), channel_id=1, source_target_pairs={{0,4},{4,0},{1,5},{5,1},{2,6},{6,2},{3,7},{7,3}} | collective-permute-start | bytes 6291464 | tf_op jit(solution)/shard_map/ppermute | solution.py:329
  1957.4 273.7 %collective-permute-start.58 = (bf16[2048,512]{1,0:T(8,128)(2,1)}, bf16[2048,512]{1,0:T(8,128)(2,1)}, u32[]{:S(2)}, u32[]{:S(2)}) collective-permute-start(bf16[2048,512]{1,0:T(8,128)(2,1)} %outer_rows.25.after_ref), channel_id=1, source_target_pairs={{0,4},{4,0},{1,5},{5,1},{2,6},{6,2},{3,7},{7,3}} | collective-permute-start | bytes 6291464 | tf_op jit(solution)/shard_map/ppermute | solution.py:329
  1965.7 265.4 %collective-permute-start.59 = (bf16[2048,512]{1,0:T(8,128)(2,1)}, bf16[2048,512]{1,0:T(8,128)(2,1)}, u32[]{:S(2)}, u32[]{:S(2)}) collective-permute-start(bf16[2048,512]{1,0:T(8,128)(2,1)} %outer_rows.26.after_ref), channel_id=1, source_target_pairs={{0,4},{4,0},{1,5},{5,1},{2,6},{6,2},{3,7},{7,3}} | collective-permute-start | bytes 6291464 | tf_op jit(solution)/shard_map/ppermute | solution.py:329
  (42 other events, 2642.8 us)
